TPU v7x, 512 devices: a 4x2x32 block of a 4x8x32 slice. The times are simulated.
512 devices in a mesh: groups: 2 (over y), seq: 32 (over z), batch: 4 (over x), head: 2 (over core).
Axes of the slice: x: 4, y: 2, z: 32, core: 2. Of those that a mesh axis runs over, the one named last changes fastest.
The devices are a block of a 4x8x32 slice.
Arguments:
- query_in: bfloat16 [8, 16384, 1024], P(('groups', 'batch'), 'seq', 'head'), parts along dimension 0, may hold values from -1.5 to 1.5
- key_in: bfloat16 [8, 16384, 1024], P(('groups', 'batch'), 'seq', 'head'), parts along dimension 0, may hold values from -1.5 to 1.5
- value_in: bfloat16 [8, 16384, 1024], P(('groups', 'batch'), 'seq', 'head'), parts along dimension 0, may hold values from -6 to 6
- level_mask: int32 [8, 16384, 16], P(('groups', 'batch'), 'seq'), parts along dimension 0, may hold values 0 or 1
- out_weight: bfloat16 [1024, 2048], P('head'), may hold values from -0.1875 to 0.1875
- grad_out: bfloat16 [8, 16384, 2048], P(('groups', 'batch'), 'seq', 'head'), parts along dimension 0, may hold values from -0.8984375 to 0.8984375
Outputs:
- layer_out: bfloat16 [8, 16384, 2048], P(('groups', 'batch'), 'seq', 'head'), parts along dimension 0
- grad_query: bfloat16 [8, 16384, 1024], P(('groups', 'batch'), 'seq', 'head'), parts along dimension 0
- grad_key: bfloat16 [8, 16384, 1024], P(('groups', 'batch'), 'seq', 'head'), parts along dimension 0
- grad_value: bfloat16 [8, 16384, 1024], P(('groups', 'batch'), 'seq', 'head'), parts along dimension 0
There are 2 independent parts, one for each index of `groups`. A program takes and returns all parts, laid end to end along the dimension named above; an argument that names none is the same for every part. Nothing has to cross between parts.
All inputs are finite; a program needn't handle non-finite values. No bound on the sum of `level_mask` on one device may be relied on, other than what follows from the above.
Results may differ from a plain program's by a relative error of at most 0.0091.
Values may be sent and summed in bfloat16 or wider, within the bound.
A program may use at most 64 MiB of HBM per device.

v0:
```python
import jax
import jax.numpy as jnp
import numpy as np
from jax import lax
from jax.sharding import PartitionSpec as P

HEAD_DIM = 128


level_scale = np.array(
    [1.0] + [2.0 ** (-(tier - 1) / 2.0) for tier in range(1, 16)], dtype=np.float32
)
HIGHEST = lax.Precision.HIGHEST


def from_partner(block, axis, stride):
    count = lax.axis_size(axis)
    route = []
    for low in range(count):
        high = low | 1 << stride
        if high != low and high < count:
            route += [(low, high), (high, low)]
    return lax.ppermute(block, axis, route)


def in_order(pieces, dim):
    pieces = jnp.moveaxis(pieces, 0, dim)
    lengths = pieces.shape
    return pieces.reshape(*lengths[:dim], lengths[dim] * lengths[dim + 1], *lengths[dim + 2 :])


def copy_for_each(shard, axis):
    copies = jnp.broadcast_to(shard, (lax.axis_size(axis), *shard.shape))
    return lax.all_to_all(copies, axis, split_axis=0, concat_axis=0, tiled=True)


def gathered_copies(shard, axis, dim):
    return in_order(copy_for_each(shard, axis), dim)


def split_up(shard, dim, peers):
    lengths = shard.shape
    pieces = shard.reshape(*lengths[:dim], peers, lengths[dim] // peers, *lengths[dim + 1 :])
    return jnp.moveaxis(pieces, dim, 0)


def sent_and_summed(shard, axis, dim):
    pieces = split_up(shard, dim, lax.axis_size(axis))
    arrived = lax.all_to_all(pieces, axis, split_axis=0, concat_axis=0, tiled=True)
    return arrived.astype(jnp.float32).sum(axis=0)


def top_bit(values):
    result = jnp.zeros_like(values)
    for power in range(1, 24):
        result = result + (values >= 1 << power).astype(jnp.int32)
    return result


def block_levels(count):
    rows = jnp.arange(count, dtype=jnp.int32)
    later = rows[:, None]
    earlier = rows[None, :]
    spread = jnp.bitwise_xor(later, earlier)
    depth_map = jnp.where(spread == 0, 0, 1 + top_bit(jnp.maximum(spread, 1)))
    inside = earlier <= later
    return jnp.stack(
        [((depth_map == tier) & inside).astype(jnp.float32) for tier in range(count.bit_length())]
    )


def reverse_tree(reach, position, span):
    back = jnp.zeros_like(reach[0])
    pending = reach
    for bit_pos in range(span):
        other_up = from_partner(pending.astype(jnp.bfloat16), "seq", bit_pos).astype(pending.dtype)
        lower = position >> bit_pos & 1 == 0
        back = back + jnp.where(lower, other_up[0], 0.0)
        pending = pending[1:] + other_up[1:]
    return back


def on_device(query_in, key_in, value_in, level_mask, out_weight, grad_out):
    batch_rows, length, width = query_in.shape
    heads = width // HEAD_DIM
    shape_heads = (batch_rows, length, heads, HEAD_DIM)
    query_rows = query_in.reshape(shape_heads)
    key_rows = key_in.reshape(shape_heads)
    value_rows = value_in.reshape(shape_heads)
    weights = level_mask.astype(jnp.float32) * jnp.asarray(level_scale, dtype=jnp.float32)
    tiers = length.bit_length()
    span = lax.axis_size("seq").bit_length() - 1
    position = lax.axis_index("seq")
    tier_weight = weights[:, :, tiers : tiers + span]
    grad_mixed = jnp.einsum(
        "bte,fe->btf",
        gathered_copies(grad_out, "head", 2),
        out_weight,
        preferred_element_type=jnp.float32,
    ).astype(jnp.bfloat16)
    grad_rows = grad_mixed.reshape(shape_heads)
    block_state = jnp.einsum(
        "bthd,bthe->bhde", key_rows, value_rows, preferred_element_type=jnp.float32
    )
    weighted_query = (
        jnp.transpose(tier_weight, (2, 0, 1))[:, :, :, None, None] * query_rows[None]
    ).astype(jnp.bfloat16)
    reach = jnp.einsum(
        "jbthd,bthe->jbhde", weighted_query, grad_rows, preferred_element_type=jnp.float32
    )
    rising = block_state
    collected = []
    for bit_pos in range(span):
        other = from_partner(rising.astype(jnp.bfloat16), "seq", bit_pos).astype(rising.dtype)
        upper = position >> bit_pos & 1 == 1
        collected.append(jnp.where(upper, other, 0.0))
        rising = rising + other
    states = jnp.stack(collected)
    back = reverse_tree(reach, position, span)
    states_low = states.astype(jnp.bfloat16)
    back_low = back.astype(jnp.bfloat16)
    intra_map = block_levels(length)
    blend = jnp.einsum("lts,btl->bts", intra_map, weights[:, :, :tiers], precision=HIGHEST)
    scores = jnp.einsum("bthd,bshd->bhts", query_rows, key_rows, preferred_element_type=jnp.float32)
    probs = (scores * blend[:, None]).astype(jnp.bfloat16)
    local_out = jnp.einsum("bhts,bshd->bthd", probs, value_rows, preferred_element_type=jnp.float32)
    far_out = jnp.einsum(
        "jbthd,jbhde->bthe", weighted_query, states_low, preferred_element_type=jnp.float32
    )
    mixed = (local_out + far_out).astype(jnp.bfloat16).reshape(batch_rows, length, width)
    partial_out = jnp.einsum("btf,fe->bte", mixed, out_weight, preferred_element_type=jnp.float32)
    layer_out = sent_and_summed(partial_out.astype(jnp.bfloat16), "head", 2).astype(jnp.bfloat16)
    dprob = jnp.einsum("bthe,bshe->bhts", grad_rows, value_rows, preferred_element_type=jnp.float32)
    dscore = (dprob * blend[:, None]).astype(jnp.bfloat16)
    query_local = jnp.einsum(
        "bhts,bshd->bthd", dscore, key_rows, preferred_element_type=jnp.float32
    )
    key_local = jnp.einsum(
        "bhts,bthd->bshd", dscore, query_rows, preferred_element_type=jnp.float32
    )
    value_local = jnp.einsum(
        "bhts,bthe->bshe", probs, grad_rows, preferred_element_type=jnp.float32
    )
    per_level = jnp.einsum(
        "bthe,jbhde->jbthd", grad_rows, states_low, preferred_element_type=jnp.float32
    )
    query_far = jnp.einsum("btj,jbthd->bthd", tier_weight, per_level, precision=HIGHEST)
    key_far = jnp.einsum(
        "bhde,bshe->bshd", back_low, value_rows, preferred_element_type=jnp.float32
    )
    value_far = jnp.einsum(
        "bhde,bshd->bshe", back_low, key_rows, preferred_element_type=jnp.float32
    )
    flat = (batch_rows, length, width)
    grad_query = (query_local + query_far).astype(jnp.bfloat16).reshape(flat)
    grad_key = (key_local + key_far).astype(jnp.bfloat16).reshape(flat)
    grad_value = (value_local + value_far).astype(jnp.bfloat16).reshape(flat)
    return (layer_out, grad_query, grad_key, grad_value)


def solution(mesh):
    return jax.shard_map(
        on_device,
        mesh=mesh,
        in_specs=(
            P(("groups", "batch"), "seq", "head"),
            P(("groups", "batch"), "seq", "head"),
            P(("groups", "batch"), "seq", "head"),
            P(("groups", "batch"), "seq", None),
            P("head", None),
            P(("groups", "batch"), "seq", "head"),
        ),
        out_specs=(
            P(("groups", "batch"), "seq", "head"),
            P(("groups", "batch"), "seq", "head"),
            P(("groups", "batch"), "seq", "head"),
            P(("groups", "batch"), "seq", "head"),
        ),
        check_vma=False,
    )
```

profile of v0, /device:TPU:45, one launch (start us, length us, event | category | flops | bytes accessed | tf_op | source)
XLA Modules:
  0.0 323.3 jit_solution(3953275357661487033)
XLA Ops:
  3.7 5.6 %all-to-all-start.1 = ((bf16[2,1,512,1024]{2,3,1,0:T(8,128)(2,1)}), bf16[2,1,512,1024]{2,3,1,0:T(8,128)(2,1)}, u32[]{:S(2)}, u32[]{:S(2)}) async-start(bf16[2,1,512,1024]{2,3,1,0:T(8,128)(2,1)} %broadcast_in_dim.25), calls=%async_computation.1 | async-start | bytes 4194304 | tf_op jit(solution)/shard_map/all_to_all | solution.py:34
  11.9 2.9 convolution_convert_fusion.1
  14.9 2.3 fusion.97
  17.2 4.4 %collective-permute-start.5 = (bf16[5,1,4,128,128]{3,4,0,2,1:T(8,128)(2,1)}, bf16[5,1,4,128,128]{3,4,0,2,1:T(8,128)(2,1)}, u32[]{:S(2)}, u32[]{:S(2)}) collective-permute-start(bf16[5,1,4,128,128]{3,4,0,2,1:T(8,128)(2,1)} %get-tuple-element.24), channel_id=1, source_target_pairs={{0,8},{8,0},{16,24},{24,16},{32,40},{40,32},{48,56},{56,48},{64,72... | collective-permute-start | bytes 1966088 | tf_op jit(solution)/shard_map/ppermute | solution.py:23
  30.8 2.1 copy.66
  47.4 7.8 %fusion = f32[512,1,512]{2,1,0:T(1,128)S(1)} fusion(f32[512,10,1]{1,2,0:T(1,128)} %copy.73, pred[10,512,512]{2,1,0:T(8,128)(4,1)} %fusion.64), kind=kOutput, calls=%fused_computation | convolution fusion | flops 31457280 | bytes 3690496 | tf_op jit(solution)/shard_map/lts,btl->bts/dot_general | solution.py:123
  60.9 6.8 %collective-permute-start.1 = (bf16[1,4,128,128]{3,2,1,0:T(8,128)(2,1)S(1)}, bf16[1,4,128,128]{3,2,1,0:T(8,128)(2,1)S(1)}, u32[]{:S(2)}, u32[]{:S(2)}) collective-permute-start(bf16[1,4,128,128]{3,2,1,0:T(8,128)(2,1)S(1)} %fusion.84), channel_id=1, source_target_pairs={{0,16},{16,0},{8,24},{24,8},{32,48},{48,32},{40,56},{56,40},{64,80... | collective-permute-start | bytes 393224 | tf_op jit(solution)/shard_map/ppermute | solution.py:23
  67.7 6.0 %collective-permute-done.1 = bf16[1,4,128,128]{3,2,1,0:T(8,128)(2,1)S(1)} collective-permute-done((bf16[1,4,128,128]{3,2,1,0:T(8,128)(2,1)S(1)}, bf16[1,4,128,128]{3,2,1,0:T(8,128)(2,1)S(1)}, u32[]{:S(2)}, u32[]{:S(2)}) %collective-permute-start.1) | collective-permute-done | bytes 131104 | tf_op jit(solution)/shard_map/ppermute | solution.py:23
  73.7 12.3 %collective-permute-start.2 = (bf16[1,4,128,128]{3,2,1,0:T(8,128)(2,1)S(1)}, bf16[1,4,128,128]{3,2,1,0:T(8,128)(2,1)S(1)}, u32[]{:S(2)}, u32[]{:S(2)}) collective-permute-start(bf16[1,4,128,128]{3,2,1,0:T(8,128)(2,1)S(1)} %fusion.93), channel_id=1, source_target_pairs={{0,32},{32,0},{8,40},{40,8},{16,48},{48,16},{24,56},{56,24},{64,96... | collective-permute-start | bytes 393224 | tf_op jit(solution)/shard_map/ppermute | solution.py:23
  86.1 11.0 %collective-permute-done.2 = bf16[1,4,128,128]{3,2,1,0:T(8,128)(2,1)S(1)} collective-permute-done((bf16[1,4,128,128]{3,2,1,0:T(8,128)(2,1)S(1)}, bf16[1,4,128,128]{3,2,1,0:T(8,128)(2,1)S(1)}, u32[]{:S(2)}, u32[]{:S(2)}) %collective-permute-start.2) | collective-permute-done | bytes 131104 | tf_op jit(solution)/shard_map/ppermute | solution.py:23
  97.1 23.8 %collective-permute-start.3 = (bf16[1,4,128,128]{3,2,1,0:T(8,128)(2,1)S(1)}, bf16[1,4,128,128]{3,2,1,0:T(8,128)(2,1)S(1)}, u32[]{:S(2)}, u32[]{:S(2)}) collective-permute-start(bf16[1,4,128,128]{3,2,1,0:T(8,128)(2,1)S(1)} %fusion.85), channel_id=1, source_target_pairs={{0,64},{64,0},{8,72},{72,8},{16,80},{80,16},{24,88},{88,24},{32,96... | collective-permute-start | bytes 393224 | tf_op jit(solution)/shard_map/ppermute | solution.py:23
  124.3 14.3 %collective-permute-done.3 = bf16[1,4,128,128]{3,2,1,0:T(8,128)(2,1)S(1)} collective-permute-done((bf16[1,4,128,128]{3,2,1,0:T(8,128)(2,1)S(1)}, bf16[1,4,128,128]{3,2,1,0:T(8,128)(2,1)S(1)}, u32[]{:S(2)}, u32[]{:S(2)}) %collective-permute-start.3) | collective-permute-done | bytes 131104 | tf_op jit(solution)/shard_map/ppermute | solution.py:23
  138.7 25.3 %collective-permute-start.4 = (bf16[1,4,128,128]{3,2,1,0:T(8,128)(2,1)S(1)}, bf16[1,4,128,128]{3,2,1,0:T(8,128)(2,1)S(1)}, u32[]{:S(2)}, u32[]{:S(2)}) collective-permute-start(bf16[1,4,128,128]{3,2,1,0:T(8,128)(2,1)S(1)} %fusion.77), channel_id=1, source_target_pairs={{0,128},{128,0},{8,136},{136,8},{16,144},{144,16},{24,152},{152,24... | collective-permute-start | bytes 393224 | tf_op jit(solution)/shard_map/ppermute | solution.py:23
  166.4 3.8 %collective-permute-done.4 = bf16[1,4,128,128]{3,2,1,0:T(8,128)(2,1)S(1)} collective-permute-done((bf16[1,4,128,128]{3,2,1,0:T(8,128)(2,1)S(1)}, bf16[1,4,128,128]{3,2,1,0:T(8,128)(2,1)S(1)}, u32[]{:S(2)}, u32[]{:S(2)}) %collective-permute-start.4) | collective-permute-done | bytes 131104 | tf_op jit(solution)/shard_map/ppermute | solution.py:23
  171.6 50.7 %collective-permute-done.7 = bf16[3,1,4,128,128]{3,4,0,2,1:T(8,128)(2,1)S(1)} collective-permute-done((bf16[3,1,4,128,128]{3,4,0,2,1:T(8,128)(2,1)S(1)}, bf16[3,1,4,128,128]{3,4,0,2,1:T(8,128)(2,1)S(1)}, u32[]{:S(2)}, u32[]{:S(2)}) %collective-permute-start.7) | collective-permute-done | bytes 393248 | tf_op jit(solution)/shard_map/ppermute | solution.py:23
  224.5 2.6 convolution_convert_fusion
  228.0 35.5 %collective-permute-done.8 = bf16[2,1,4,128,128]{3,4,0,2,1:T(8,128)(2,1)S(1)} collective-permute-done((bf16[2,1,4,128,128]{3,4,0,2,1:T(8,128)(2,1)S(1)}, bf16[2,1,4,128,128]{3,4,0,2,1:T(8,128)(2,1)S(1)}, u32[]{:S(2)}, u32[]{:S(2)}) %collective-permute-start.8) | collective-permute-done | bytes 262176 | tf_op jit(solution)/shard_map/ppermute | solution.py:23
  263.5 30.8 %collective-permute-start.9 = (bf16[1,1,4,128,128]{3,4,0,2,1:T(8,128)(2,1)S(1)}, bf16[1,1,4,128,128]{3,4,0,2,1:T(8,128)(2,1)S(1)}, u32[]{:S(2)}, u32[]{:S(2)}) collective-permute-start(bf16[1,1,4,128,128]{3,4,0,2,1:T(8,128)(2,1)S(1)} %fusion.78), channel_id=1, source_target_pairs={{0,128},{128,0},{8,136},{136,8},{16,144},{144,16},{24,152},{152,24... | collective-permute-start | bytes 393224 | tf_op jit(solution)/shard_map/ppermute | solution.py:23
  295.9 2.0 copy.70
  298.0 4.5 %reshape.703 = bf16[1,512,2,1024]{3,2,1,0:T(2,128)(2,1)} reshape(bf16[512,2048]{1,0:T(8,128)(2,1)} %convolution_convert_fusion) | data formatting | bytes 4194304 | tf_op jit(solution)/shard_map/reshape | solution.py:43
  302.5 2.2 copy.115
  304.7 7.0 %all_to_all.10 = bf16[2,1,512,1024]{3,2,1,0:T(8,128)(2,1)} all-to-all(bf16[2,1,512,1024]{3,2,1,0:T(8,128)(2,1)S(1)} %bitcast.142), channel_id=1, replica_groups=mesh['groups'=2,'seq'=32,'batch'=4,'head'=2] {'head'}, dimensions={0} | all-to-all | bytes 4194304 | tf_op jit(solution)/shard_map/all_to_all | solution.py:49
  311.7 3.3 %reduce_sum.14 = bf16[512,1024]{1,0:T(8,128)(2,1)} reduce(bf16[2,1,512,1024]{3,2,1,0:T(8,128)(2,1)} %all_to_all.10, bf16[]{:T(256)} %constant.33.clone.1), dimensions={0,1}, to_apply=%region_0.1 | reduce | flops 524288 | bytes 3145730 | tf_op jit(solution)/shard_map/reduce_sum | solution.py:50
  316.3 2.3 fusion.18
  (100 shorter events, 52.8 us)
Async XLA Ops:
  0.6 11.3 %copy-start = (bf16[512,2048]{1,0:T(8,128)(2,1)S(1)}, bf16[512,2048]{1,0:T(8,128)(2,1)}, u32[]{:S(2)}) copy-start(bf16[512,2048]{1,0:T(8,128)(2,1)} %param.11) | copy-start | bytes 6291460
  3.7 5.6 %copy-start.16 = (s32[1,512,16]{1,2,0:T(8,128)S(1)}, s32[1,512,16]{1,2,0:T(8,128)}, u32[]{:S(2)}) copy-start(s32[1,512,16]{1,2,0:T(8,128)} %param.10) | copy-start | bytes 98308
  3.7 5.6 %copy-start.18 = (f32[16]{0:T(128)S(1)}, f32[16]{0:T(128)}, u32[]{:S(2)}) copy-start(f32[16]{0:T(128)} %constant.34.clone) | copy-start | bytes 196
  3.7 6.9 %copy-start.13 = (bf16[1,512,512]{2,1,0:T(8,128)(2,1)S(1)}, bf16[1,512,512]{2,1,0:T(8,128)(2,1)}, u32[]{:S(2)}) copy-start(bf16[1,512,512]{2,1,0:T(8,128)(2,1)} %param.7) | copy-start | bytes 1572868
  3.7 8.2 %all-to-all-start.1 = ((bf16[2,1,512,1024]{2,3,1,0:T(8,128)(2,1)}), bf16[2,1,512,1024]{2,3,1,0:T(8,128)(2,1)}, u32[]{:S(2)}, u32[]{:S(2)}) async-start(bf16[2,1,512,1024]{2,3,1,0:T(8,128)(2,1)} %broadcast_in_dim.25), calls=%async_computation.1 | async-start | bytes 4194304 | tf_op jit(solution)/shard_map/all_to_all | solution.py:34
  14.9 6.7 %copy-start.14 = (bf16[1,512,512]{2,1,0:T(8,128)(2,1)S(1)}, bf16[1,512,512]{2,1,0:T(8,128)(2,1)}, u32[]{:S(2)}) copy-start(bf16[1,512,512]{2,1,0:T(8,128)(2,1)} %param.8) | copy-start | bytes 1572868
  17.2 103.7 %collective-permute-start.5 = (bf16[5,1,4,128,128]{3,4,0,2,1:T(8,128)(2,1)}, bf16[5,1,4,128,128]{3,4,0,2,1:T(8,128)(2,1)}, u32[]{:S(2)}, u32[]{:S(2)}) collective-permute-start(bf16[5,1,4,128,128]{3,4,0,2,1:T(8,128)(2,1)} %get-tuple-element.24), channel_id=1, source_target_pairs={{0,8},{8,0},{16,24},{24,16},{32,40},{40,32},{48,56},{56,48},{64,72... | collective-permute-start | bytes 1966088 | tf_op jit(solution)/shard_map/ppermute | solution.py:23
  26.1 34.8 %collective-permute-start = (bf16[1,4,128,128]{3,2,1,0:T(8,128)(2,1)}, bf16[1,4,128,128]{3,2,1,0:T(8,128)(2,1)S(1)}, u32[]{:S(2)}, u32[]{:S(2)}) collective-permute-start(bf16[1,4,128,128]{3,2,1,0:T(8,128)(2,1)} %convert_bitcast_fusion), channel_id=1, source_target_pairs={{0,8},{8,0},{16,24},{24,16},{32,40},{40,32},{48,56},{56,48},{64,72... | collective-permute-start | bytes 393224 | tf_op jit(solution)/shard_map/ppermute | solution.py:23
  47.4 7.9 %copy-start.5 = (bf16[512,4,128]{0,2,1:T(8,128)(2,1)S(1)}, bf16[512,4,128]{0,2,1:T(8,128)(2,1)}, u32[]{:S(2)}) copy-start(bf16[512,4,128]{0,2,1:T(8,128)(2,1)} %copy.66) | copy-start | bytes 1572868
  60.8 61.3 %copy-start.7 = (f32[5,1,4,128,128]{3,4,0,2,1:T(8,128)S(1)}, f32[5,1,4,128,128]{3,4,0,2,1:T(8,128)}, u32[]{:S(2)}) copy-start(f32[5,1,4,128,128]{3,4,0,2,1:T(8,128)} %get-tuple-element.25) | copy-start | bytes 3932164
  60.9 12.8 %collective-permute-start.1 = (bf16[1,4,128,128]{3,2,1,0:T(8,128)(2,1)S(1)}, bf16[1,4,128,128]{3,2,1,0:T(8,128)(2,1)S(1)}, u32[]{:S(2)}, u32[]{:S(2)}) collective-permute-start(bf16[1,4,128,128]{3,2,1,0:T(8,128)(2,1)S(1)} %fusion.84), channel_id=1, source_target_pairs={{0,16},{16,0},{8,24},{24,8},{32,48},{48,32},{40,56},{56,40},{64,80... | collective-permute-start | bytes 393224 | tf_op jit(solution)/shard_map/ppermute | solution.py:23
  73.7 23.3 %collective-permute-start.2 = (bf16[1,4,128,128]{3,2,1,0:T(8,128)(2,1)S(1)}, bf16[1,4,128,128]{3,2,1,0:T(8,128)(2,1)S(1)}, u32[]{:S(2)}, u32[]{:S(2)}) collective-permute-start(bf16[1,4,128,128]{3,2,1,0:T(8,128)(2,1)S(1)} %fusion.93), channel_id=1, source_target_pairs={{0,32},{32,0},{8,40},{40,8},{16,48},{48,16},{24,56},{56,24},{64,96... | collective-permute-start | bytes 393224 | tf_op jit(solution)/shard_map/ppermute | solution.py:23
  97.1 41.5 %collective-permute-start.3 = (bf16[1,4,128,128]{3,2,1,0:T(8,128)(2,1)S(1)}, bf16[1,4,128,128]{3,2,1,0:T(8,128)(2,1)S(1)}, u32[]{:S(2)}, u32[]{:S(2)}) collective-permute-start(bf16[1,4,128,128]{3,2,1,0:T(8,128)(2,1)S(1)} %fusion.85), channel_id=1, source_target_pairs={{0,64},{64,0},{8,72},{72,8},{16,80},{80,16},{24,88},{88,24},{32,96... | collective-permute-start | bytes 393224 | tf_op jit(solution)/shard_map/ppermute | solution.py:23
  122.1 42.1 %copy-start.1 = (f32[5,1,4,128,128]{3,4,0,2,1:T(8,128)}, f32[5,1,4,128,128]{3,4,0,2,1:T(8,128)S(1)}, u32[]{:S(2)}) copy-start(f32[5,1,4,128,128]{3,4,0,2,1:T(8,128)S(1)} %convert_element_type.1727) | copy-start | bytes 3932164
  122.3 41.8 %collective-permute-start.6 = (bf16[4,1,4,128,128]{3,4,0,2,1:T(8,128)(2,1)S(1)}, bf16[4,1,4,128,128]{3,4,0,2,1:T(8,128)(2,1)S(1)}, u32[]{:S(2)}, u32[]{:S(2)}) collective-permute-start(bf16[4,1,4,128,128]{3,4,0,2,1:T(8,128)(2,1)S(1)} %get-tuple-element.20), channel_id=1, source_target_pairs={{0,16},{16,0},{8,24},{24,8},{32,48},{48,32},{40,56},{56,40},{64,80... | collective-permute-start | bytes 1572872 | tf_op jit(solution)/shard_map/ppermute | solution.py:23
  138.7 31.5 %copy-start.9 = (f32[512,4,128]{2,0,1:T(8,128)S(1)}, f32[512,4,128]{2,0,1:T(8,128)}, u32[]{:S(2)}) copy-start(f32[512,4,128]{2,0,1:T(8,128)} %copy.55) | copy-start | bytes 3145732
  138.7 31.4 %collective-permute-start.4 = (bf16[1,4,128,128]{3,2,1,0:T(8,128)(2,1)S(1)}, bf16[1,4,128,128]{3,2,1,0:T(8,128)(2,1)S(1)}, u32[]{:S(2)}, u32[]{:S(2)}) collective-permute-start(bf16[1,4,128,128]{3,2,1,0:T(8,128)(2,1)S(1)} %fusion.77), channel_id=1, source_target_pairs={{0,128},{128,0},{8,136},{136,8},{16,144},{144,16},{24,152},{152,24... | collective-permute-start | bytes 393224 | tf_op jit(solution)/shard_map/ppermute | solution.py:23
  164.3 7.3 %copy-start.10 = (f32[4,1,4,128,128]{3,4,0,2,1:T(8,128)}, f32[4,1,4,128,128]{3,4,0,2,1:T(8,128)S(1)}, u32[]{:S(2)}) copy-start(f32[4,1,4,128,128]{3,4,0,2,1:T(8,128)S(1)} %convert_element_type.1729) | copy-start | bytes 3145732
  164.4 57.9 %collective-permute-start.7 = (bf16[3,1,4,128,128]{3,4,0,2,1:T(8,128)(2,1)S(1)}, bf16[3,1,4,128,128]{3,4,0,2,1:T(8,128)(2,1)S(1)}, u32[]{:S(2)}, u32[]{:S(2)}) collective-permute-start(bf16[3,1,4,128,128]{3,4,0,2,1:T(8,128)(2,1)S(1)} %get-tuple-element.18), channel_id=1, source_target_pairs={{0,32},{32,0},{8,40},{40,8},{16,48},{48,16},{24,56},{56,24},{64,96... | collective-permute-start | bytes 1179656 | tf_op jit(solution)/shard_map/ppermute | solution.py:23
  222.4 4.7 %copy-start.11 = (f32[3,1,4,128,128]{3,4,0,2,1:T(8,128)}, f32[3,1,4,128,128]{3,4,0,2,1:T(8,128)S(1)}, u32[]{:S(2)}) copy-start(f32[3,1,4,128,128]{3,4,0,2,1:T(8,128)S(1)} %convert_element_type.1731) | copy-start | bytes 2359300
  222.5 41.0 %collective-permute-start.8 = (bf16[2,1,4,128,128]{3,4,0,2,1:T(8,128)(2,1)S(1)}, bf16[2,1,4,128,128]{3,4,0,2,1:T(8,128)(2,1)S(1)}, u32[]{:S(2)}, u32[]{:S(2)}) collective-permute-start(bf16[2,1,4,128,128]{3,4,0,2,1:T(8,128)(2,1)S(1)} %get-tuple-element.16), channel_id=1, source_target_pairs={{0,64},{64,0},{8,72},{72,8},{16,80},{80,16},{24,88},{88,24},{32,96... | collective-permute-start | bytes 786440 | tf_op jit(solution)/shard_map/ppermute | solution.py:23
  227.1 67.2 %copy-start.6 = (bf16[512,4,128]{0,2,1:T(8,128)(2,1)S(1)}, bf16[512,4,128]{0,2,1:T(8,128)(2,1)}, u32[]{:S(2)}) copy-start(bf16[512,4,128]{0,2,1:T(8,128)(2,1)} %copy.53) | copy-start | bytes 1572868
  263.5 32.4 %copy-start.12 = (f32[2,1,4,128,128]{3,4,0,2,1:T(8,128)}, f32[2,1,4,128,128]{3,4,0,2,1:T(8,128)S(1)}, u32[]{:S(2)}) copy-start(f32[2,1,4,128,128]{3,4,0,2,1:T(8,128)S(1)} %convert_element_type.1733) | copy-start | bytes 1572868
  263.5 51.5 %collective-permute-start.9 = (bf16[1,1,4,128,128]{3,4,0,2,1:T(8,128)(2,1)S(1)}, bf16[1,1,4,128,128]{3,4,0,2,1:T(8,128)(2,1)S(1)}, u32[]{:S(2)}, u32[]{:S(2)}) collective-permute-start(bf16[1,1,4,128,128]{3,4,0,2,1:T(8,128)(2,1)S(1)} %fusion.78), channel_id=1, source_target_pairs={{0,128},{128,0},{8,136},{136,8},{16,144},{144,16},{24,152},{152,24... | collective-permute-start | bytes 393224 | tf_op jit(solution)/shard_map/ppermute | solution.py:23
  (6 other events, 13.7 us)
where the time goes:
time: 325 us; the launch traced here: 323 us
  waiting for transfers between devices  121 us (37%)
  starting transfers between devices  117 us (36%)
  matrix products  29.9 us (9%)
  local copies, waits for them, and re-layouts  25.2 us (8%)
  other arithmetic  21.9 us (7%)
  blocking collectives  7.01 us (2%)
    ppermute x10, waiting for transfers between devices, from_partner(): return lax.ppermute(block, axis, route)  121 us
    ppermute x10, starting transfers between devices, from_partner(): return lax.ppermute(block, axis, route)  111 us
    unnamed x13, other arithmetic  13.1 us
    dot_general x1, matrix products, on_device(): jnp.einsum('lts,btl->bts', intra_map, weights[:, :, :tiers], precision=HI...  7.82 us
    another operation x7, local copies, waits for them, and re-layouts  7.61 us
    all_to_all x1, blocking collectives, sent_and_summed(): lax.all_to_all(pieces, axis, split_axis=0, concat_axis=0, tiled=True)  7.01 us
    reshape x2, local copies, waits for them, and re-layouts, split_up(): shard.reshape(*lengths[:dim], peers, lengths[dim] // peers, *lengths[dim...  6.7 us
  transfers between devices with their start and end apart: 11, of which 7 were waited for; matrix products, arithmetic and copies ran while one was open for 18% of the time, Pallas kernels for 0%

commit v1 on v0

v1 whole, which is shorter than its diff:
```python
import functools

import jax
import jax.numpy as jnp
import numpy as np
from jax import lax
from jax.experimental import pallas as pl
from jax.experimental.pallas import tpu as pltpu
from jax.sharding import PartitionSpec as P

MESH = pl.DeviceIdType.MESH
HD = 128
F32 = jnp.float32
BF16 = jnp.bfloat16
ROOT_HALF = float(np.float32(2.0**-0.5))


def tier_scale(tier):
    return 1.0 if tier == 0 else float(np.float32(2.0 ** (-(tier - 1) / 2.0)))


def nn(a, b):
    return lax.dot_general(a, b, (((1,), (0,)), ((), ())), preferred_element_type=F32)


def nt(a, b):
    return lax.dot_general(a, b, (((1,), (1,)), ((), ())), preferred_element_type=F32)


def tn(a, b):
    return lax.dot_general(a, b, (((0,), (0,)), ((), ())), preferred_element_type=F32)


def kernel(
    n_seq, heads, length, half_d,
    q_hbm, k_hbm, v_hbm, m_hbm, w_hbm, go_hbm,
    lay_hbm, gq_hbm, gk_hbm, gv_hbm,
    qv, kv, vv, mv, wv, go, gop, wp,
    blend, mb, gacc, gm, state, fr, agg, reach, out, br, total,
    lo, ql, kl, vl, mix, mixp, lay, gq, gk, gv,
    in_sem, out_sem, hs_send, hs_recv, mx_send, mx_recv, fs, fr_sem, bs, br_sem,
):
    n = lax.axis_index("seq")
    core = lax.axis_index("head")
    other = 1 - core
    span = n_seq.bit_length() - 1
    tiers = length.bit_length()
    half = length // 2
    r = lax.rem(n, 4)
    up = [lax.rem(n >> j, 2) for j in range(span)]
    nxt = [lax.rem((n + 1) >> j, 2) for j in range(span)]
    last = n == n_seq - 1
    pending = []

    barrier = pltpu.get_barrier_semaphore()
    dists = (1, n_seq - 1, 2, n_seq - 2, 4, n_seq - 4)
    pl.semaphore_signal(barrier, inc=1, device_id={"head": other}, device_id_type=MESH)
    for d in dists:
        pl.semaphore_signal(
            barrier, inc=1, device_id={"seq": lax.rem(n + d, n_seq)}, device_id_type=MESH
        )

    loads = [
        pltpu.make_async_copy(src, dst, in_sem.at[i])
        for i, (src, dst) in enumerate(
            ((k_hbm.at[0], kv), (v_hbm.at[0], vv), (go_hbm.at[0], go), (w_hbm, wv),
             (m_hbm.at[0], mv), (q_hbm.at[0], qv))
        )
    ]
    for load in loads:
        load.start()
    loads[0].wait()
    loads[1].wait()

    def cols(h):
        return pl.ds(pl.multiple_of(h * HD, HD), HD)

    def state_body(h, carry):
        s = tn(kv[:, cols(h)], vv[:, cols(h)])
        state[h] = s
        agg[h] = s.astype(BF16)
        return carry

    lax.fori_loop(0, heads, state_body, 0)
    loads[2].wait()
    loads[3].wait()

    pl.semaphore_wait(barrier, 1 + len(dists))

    own_cols = pl.ds(pl.multiple_of(core * half_d, HD), half_d)
    other_cols = pl.ds(pl.multiple_of(other * half_d, HD), half_d)

    def to_core(src, dst, i):
        return pltpu.make_async_remote_copy(
            src_ref=src, dst_ref=dst, send_sem=hs_send.at[i], recv_sem=hs_recv.at[i],
            device_id={"head": other}, device_id_type=MESH,
        )

    go_copy = to_core(go, gop, 0)
    w_copy = to_core(wv.at[:, other_cols], wp, 1)
    go_copy.start()

    def fmsg(level, which, c, src, dist):
        return pltpu.make_async_remote_copy(
            src_ref=src, dst_ref=fr.at[level, c], send_sem=fs.at[level, which, c],
            recv_sem=fr_sem.at[level, c], device_id={"seq": n + dist}, device_id_type=MESH,
        )

    def fwait(level, c):
        fmsg(level, 0, c, fr.at[level, c], 0).wait_recv()

    def fsend(level, which, c, src, dist):
        fmsg(level, which, c, src, dist).start()

    def fsent(cond, level, which):
        pending.append(
            (cond, lambda: [fmsg(level, which, c, fr.at[level, c], 0).wait_send() for c in range(heads)])
        )

    def bmsg(level, slot, c, dist):
        return pltpu.make_async_remote_copy(
            src_ref=out.at[level, c], dst_ref=br.at[level, slot, c], send_sem=bs.at[level, c],
            recv_sem=br_sem.at[level, slot, c], device_id={"seq": n - dist}, device_id_type=MESH,
        )

    def bwait(level, slot, c):
        bmsg(level, slot, c, 0).wait_recv()

    even = lax.rem(r, 2) == 0

    @pl.when(even)
    def _():
        for c in range(heads):
            fsend(0, 1, c, agg.at[c], 1)

    w_copy.start()

    def gm_body(source, weight_cols, finish):
        def body(i, carry):
            rows = pl.ds(pl.multiple_of(lax.rem(i, 2) * half, half), half)
            wide = heads * HD // 2
            feats = pl.ds(pl.multiple_of(i // 2 * wide, wide), wide)
            part = nt(source[rows, :], wv[feats, weight_cols])
            if finish:
                gm[rows, feats] = (gacc[rows, feats] + part).astype(BF16)
            else:
                gacc[rows, feats] = part
            return carry

        lax.fori_loop(0, 4, body, 0)

    gm_body(go, own_cols, False)

    @pl.when(r == 1)
    def _():
        for c in range(heads):
            fwait(0, c)
            agg[c] = (state[c] + fr[0, c].astype(F32)).astype(BF16)
            fsend(1, 0, c, agg.at[c], 2)
            fsend(1, 1, c, agg.at[c], 1)

    @pl.when(r == 3)
    def _():
        for c in range(heads):
            fwait(0, c)
            state[c] = state[c] + fr[0, c].astype(F32)

    loads[4].wait()
    loads[5].wait()

    for j in range(span):
        mb[j] = jnp.broadcast_to(mv[:, tiers + j : tiers + j + 1].astype(F32), (length, HD)).astype(BF16)

    go_copy.wait_recv()
    gm_body(gop, other_cols, True)

    def source_of(level):
        return jnp.logical_and(nxt[level] == 1, up[level] == 0)

    @pl.when(r == 3)
    def _():
        first = source_of(2)
        for c in range(heads):
            fwait(1, c)
            tot = state[c] + fr[1, c].astype(F32)
            state[c] = tot
            agg[c] = tot.astype(BF16)

            @pl.when(first)
            def _():
                fsend(2, 0, c, agg.at[c], 4)
                fsend(2, 1, c, agg.at[c], 1)

    def halves(j):
        odd = (tiers + j - 1) % 2
        return odd, 2.0 ** (-((tiers + j - 1 - odd) // 2))

    def reach_body(h, carry):
        q = qv[:, cols(h)]
        qs = (q.astype(F32) * ROOT_HALF).astype(BF16)
        g = gm[:, cols(h)]
        for j in range(span):
            odd, whole = halves(j)

            @pl.when(up[j] == 1)
            def _():
                s = tn(qs if odd else q, mb[j] * g) * whole
                reach[j, h] = s
                out[j, h] = s.astype(BF16)

        return carry

    lax.fori_loop(0, heads, reach_body, 0)

    def bsent(cond, level):
        pending.append((cond, lambda: [bmsg(level, 0, c, 0).wait_send() for c in range(heads)]))

    high = list(range(span - 1, 1, -1))
    for j in high:

        @pl.when(jnp.logical_and(r == 2, up[j] == 1))
        def _():
            for c in range(heads):
                bmsg(j, 2, c, 1).start()

        @pl.when(last)
        def _():
            for c in range(heads):
                bmsg(j, 1, c, 4).start()

    @pl.when(r == 2)
    def _():
        for c in range(heads):
            bmsg(1, 0, c, 1).start()

    @pl.when(last)
    def _():
        for c in range(heads):
            bmsg(1, 1, c, 2).start()
        for c in range(heads):
            bmsg(0, 0, c, 1).start()

    for j in range(span):
        bsent(up[j] == 1, j)

    def blend_block(rows, levels):
        t = lax.broadcasted_iota(jnp.int32, (half, half), 0)
        s = lax.broadcasted_iota(jnp.int32, (half, half), 1)
        spread = jnp.bitwise_xor(t, s)

        def column(level):
            return mv[rows, level : level + 1].astype(F32) * tier_scale(level)

        value = jnp.broadcast_to(column(0), (half, half))
        for level in range(1, levels):
            value = jnp.where(spread >= 1 << (level - 1), column(level), value)
        return jnp.where(s <= t, value, 0.0)

    top, low = pl.ds(0, half), pl.ds(half, half)
    blend[0] = blend_block(top, tiers - 1)
    blend[1] = blend_block(low, tiers - 1)
    blend[2] = jnp.broadcast_to(
        mv[low, tiers - 1 : tiers].astype(F32) * tier_scale(tiers - 1), (half, half)
    )

    def forward_step(j):
        for c in range(heads):
            fwait(j, c)

            @pl.when(r == 3)
            def _():
                @pl.when(nxt[j] == 1)
                def _():
                    fsend(j, 0, c, fr.at[j, c], 4)
                    fsend(j, 1, c, fr.at[j, c], 1)

                if j + 1 < span:

                    @pl.when(nxt[j] == 0)
                    def _():
                        tot = state[c] + fr[j, c].astype(F32)
                        state[c] = tot
                        agg[c] = tot.astype(BF16)

                        @pl.when(source_of(j + 1))
                        def _():
                            fsend(j + 1, 0, c, agg.at[c], 4)
                            fsend(j + 1, 1, c, agg.at[c], 1)

            @pl.when(r < 2)
            def _():
                fsend(j, 1, c, fr.at[j, c], 1)

    def when_forward(j, mine):
        @pl.when(jnp.logical_and(up[j] == 1, mine))
        def _():
            forward_step(j)

    def chain_step(j, position, slot):
        @pl.when(jnp.logical_and(up[j] == 1, r == position))
        def _():
            for c in range(heads):
                bwait(j, 2, c)
                out[j, c] = (reach[j, c] + br[j, 2, c].astype(F32)).astype(BF16)
                bmsg(j, slot, c, 1).start()

    def down(level):
        return {0: (0, 1), 1: (1, 2)}.get(level, (1, 4))

    def back_step(j):
        @pl.when(jnp.logical_and(r == 3, nxt[j] == 1))
        def _():
            @pl.when(up[j] == 1)
            def _():
                for c in range(heads):
                    bwait(j, 0, c)
                    bwait(j, 1, c)
                    tot = br[j, 0, c].astype(F32) + br[j, 1, c].astype(F32)
                    out[j, c] = (reach[j, c] + tot).astype(BF16)
                    bmsg(j, 1, c, 4).start()

            @pl.when(up[j] == 0)
            def _():
                for c in range(heads):
                    bwait(j, 0, c)
                    bwait(j, 1, c)
                    tot = br[j, 0, c].astype(F32) + br[j, 1, c].astype(F32)
                    total[c] = tot
                    out[j - 1, c] = (reach[j - 1, c] + tot).astype(BF16)
                    slot, dist = down(j - 1)
                    bmsg(j - 1, slot, c, dist).start()
                for level in range(j - 2, -1, -1):
                    slot, dist = down(level)
                    for c in range(heads):
                        out[level, c] = (reach[level, c] + total[c]).astype(BF16)
                        bmsg(level, slot, c, dist).start()

    def local_head(h):
        def parts(ref):
            return ref[top, cols(h)], ref[low, cols(h)]

        qa, qb = parts(qv)
        ka, kb = parts(kv)
        va, vb = parts(vv)
        ga, gb = parts(gm)
        paa = (nt(qa, ka) * blend[0]).astype(BF16)
        pba = (nt(qb, ka) * blend[2]).astype(BF16)
        pbb = (nt(qb, kb) * blend[1]).astype(BF16)
        lo[top, cols(h)] = nn(paa, va)
        lo[low, cols(h)] = nn(pba, va) + nn(pbb, vb)
        vl[top, cols(h)] = tn(paa, ga) + tn(pba, gb)
        vl[low, cols(h)] = tn(pbb, gb)
        daa = (nt(ga, va) * blend[0]).astype(BF16)
        dba = (nt(gb, va) * blend[2]).astype(BF16)
        dbb = (nt(gb, vb) * blend[1]).astype(BF16)
        ql[top, cols(h)] = nn(daa, ka)
        ql[low, cols(h)] = nn(dba, ka) + nn(dbb, kb)
        kl[top, cols(h)] = tn(daa, qa) + tn(dba, qb)
        kl[low, cols(h)] = tn(dbb, qb)

    busy = r != 2

    def local_body(i, carry):
        local_head(i)

        @pl.when(i == 0)
        def _():
            when_forward(2, busy)
            for j in high:
                chain_step(j, 1, 2)
            for j in high:
                chain_step(j, 0, 0)

        @pl.when(i == 2)
        def _():
            for j in range(3, span - 1):
                when_forward(j, busy)

        return carry

    lax.fori_loop(0, heads, local_body, 0)
    for j in high:
        back_step(j)
    when_forward(span - 1, busy)

    @pl.when(r == 1)
    def _():
        for c in range(heads):
            bwait(1, 0, c)
            bwait(1, 1, c)
            tot = br[1, 0, c].astype(F32) + br[1, 1, c].astype(F32)
            total[c] = tot
            out[0, c] = (reach[0, c] + tot).astype(BF16)
            bmsg(0, 0, c, 1).start()

    @pl.when(r == 2)
    def _():
        for j in range(1, span):

            @pl.when(up[j] == 1)
            def _():
                for c in range(heads):
                    fwait(j, c)

    for j in range(span):

        @pl.when(up[j] == 0)
        def _():
            fr[j] = jnp.zeros(fr.shape[1:], BF16)

    def mix_copy(h):
        return pltpu.make_async_remote_copy(
            src_ref=mix.at[:, cols(h)], dst_ref=mixp.at[:, cols(h)], send_sem=mx_send.at[h],
            recv_sem=mx_recv.at[h], device_id={"head": other}, device_id_type=MESH,
        )

    def far_body(h, carry):
        q = qv[:, cols(h)]
        qs = (q.astype(F32) * ROOT_HALF).astype(BF16)
        g = gm[:, cols(h)]
        mixed = lo[:, cols(h)]
        query = ql[:, cols(h)]
        for j in range(span):
            odd, whole = halves(j)
            mask = mb[j]
            st = fr[j, h]
            mixed = mixed + nn((qs if odd else q) * mask, st) * whole
            query = query + nt(mask * g, st) * tier_scale(tiers + j)
        mix[:, cols(h)] = mixed.astype(BF16)
        gq[:, cols(h)] = query.astype(BF16)
        mix_copy(h).start()
        return carry

    lax.fori_loop(0, heads, far_body, 0)

    stores = [
        pltpu.make_async_copy(src, dst, out_sem.at[i])
        for i, (src, dst) in enumerate(((gq, gq_hbm.at[0]), (gk, gk_hbm.at[0]), (gv, gv_hbm.at[0]), (lay, lay_hbm.at[0])))
    ]
    stores[0].start()

    w_copy.wait_recv()
    for h in range(heads):
        mix_copy(h).wait_recv()

    tile = 256

    def layer_body(i, carry):
        at = pl.multiple_of(i * tile, tile)
        here = pl.ds(pl.multiple_of(core * half_d + at, HD), tile)
        there = pl.ds(at, tile)
        lay[:, there] = (nn(mix[...], wv[:, here]) + nn(mixp[...], wp[:, there])).astype(BF16)
        return carry

    lax.fori_loop(0, half_d // tile, layer_body, 0)
    stores[3].start()

    @pl.when(even)
    def _():
        for c in range(heads):
            bwait(0, 0, c)
            total[c] = br[0, 0, c].astype(F32)

    @pl.when(last)
    def _():
        total[...] = jnp.zeros(total.shape, F32)

    def back_body(h, carry):
        back = total[h].astype(BF16)
        gk[:, cols(h)] = (kl[:, cols(h)] + nt(vv[:, cols(h)], back)).astype(BF16)
        gv[:, cols(h)] = (vl[:, cols(h)] + nn(kv[:, cols(h)], back)).astype(BF16)
        return carry

    lax.fori_loop(0, heads, back_body, 0)
    stores[1].start()
    stores[2].start()

    fsent(even, 0, 1)
    fsent(r == 1, 1, 0)
    fsent(r == 1, 1, 1)
    for j in range(2, span):
        sends = jnp.logical_and(r == 3, nxt[j] == 1)
        fsent(sends, j, 0)
        fsent(jnp.logical_or(sends, jnp.logical_and(r < 2, up[j] == 1)), j, 1)
    for cond, wait in pending:

        @pl.when(cond)
        def _():
            wait()

    go_copy.wait_send()
    w_copy.wait_send()
    for h in range(heads):
        mix_copy(h).wait_send()
    for store in stores:
        store.wait()


def on_device(query_in, key_in, value_in, level_mask, out_weight, grad_out):
    n_seq = lax.axis_size("seq")
    _, length, width = query_in.shape
    heads = width // HD
    half_d = grad_out.shape[2]
    span = n_seq.bit_length() - 1
    half = length // 2
    wide = lambda dtype: pltpu.VMEM((length, width), dtype)
    any_spec = pl.BlockSpec(memory_space=pl.ANY)
    dma = lambda *shape: pltpu.SemaphoreType.DMA(shape)
    layer, gq, gk, gv = pl.pallas_call(
        functools.partial(kernel, n_seq, heads, length, half_d),
        out_shape=(
            jax.ShapeDtypeStruct(grad_out.shape, BF16),
            jax.ShapeDtypeStruct(query_in.shape, BF16),
            jax.ShapeDtypeStruct(query_in.shape, BF16),
            jax.ShapeDtypeStruct(query_in.shape, BF16),
        ),
        in_specs=[any_spec] * 6,
        out_specs=(any_spec,) * 4,
        scratch_shapes=[
            wide(BF16), wide(BF16), wide(BF16),
            pltpu.VMEM(level_mask.shape[1:], jnp.int32),
            pltpu.VMEM(out_weight.shape, BF16),
            pltpu.VMEM((length, half_d), BF16),
            pltpu.VMEM((length, half_d), BF16),
            pltpu.VMEM((width, half_d), BF16),
            pltpu.VMEM((3, half, half), F32),
            pltpu.VMEM((span, length, HD), BF16),
            wide(F32), wide(BF16),
            pltpu.VMEM((heads, HD, HD), F32),
            pltpu.VMEM((span, heads, HD, HD), BF16),
            pltpu.VMEM((heads, HD, HD), BF16),
            pltpu.VMEM((span, heads, HD, HD), F32),
            pltpu.VMEM((span, heads, HD, HD), BF16),
            pltpu.VMEM((span, 3, heads, HD, HD), BF16),
            pltpu.VMEM((heads, HD, HD), F32),
            wide(F32), wide(F32), wide(F32), wide(F32),
            wide(BF16), wide(BF16),
            pltpu.VMEM((length, half_d), BF16),
            wide(BF16), wide(BF16), wide(BF16),
            dma(6), dma(4), dma(2), dma(2), dma(heads), dma(heads),
            dma(span, 2, heads), dma(span, heads), dma(span, heads), dma(span, 3, heads),
        ],
        compiler_params=pltpu.CompilerParams(collective_id=0, has_side_effects=True),
        name="log_linear",
    )(query_in, key_in, value_in, level_mask, out_weight, grad_out)
    return layer, gq, gk, gv


def solution(mesh):
    return jax.shard_map(
        on_device,
        mesh=mesh,
        in_specs=(
            P(("groups", "batch"), "seq", "head"),
            P(("groups", "batch"), "seq", "head"),
            P(("groups", "batch"), "seq", "head"),
            P(("groups", "batch"), "seq", None),
            P("head", None),
            P(("groups", "batch"), "seq", "head"),
        ),
        out_specs=(
            P(("groups", "batch"), "seq", "head"),
            P(("groups", "batch"), "seq", "head"),
            P(("groups", "batch"), "seq", "head"),
            P(("groups", "batch"), "seq", "head"),
        ),
        check_vma=False,
    )
```

time: 325 us -> 122 us (0.38)
  the two profiles are of different devices: /device:TPU:45 before, /device:TPU:97 now
where the time goes in v1:
time: 122 us; the launch traced here: 121 us
  Pallas kernels  114 us (93%)
  local copies, waits for them, and re-layouts  6.36 us (5%)
    pallas_call x1, Pallas kernels, on_device(): pl.pallas_call(functools.partial(kernel, n_seq, heads, length, half_d), o...  114 us
    unnamed x11, local copies, waits for them, and re-layouts  6.36 us

profile of v1, /device:TPU:97, one launch (start us, length us, event | category | flops | bytes accessed | tf_op | source)
XLA Modules:
  0.0 121.4 jit_solution(10485036239006147003)
XLA Ops:
  0.6 1.6 %copy.10.m_hbm = s32[1,512,16]{2,1,0:T(8,128)} copy(s32[1,512,16]{1,2,0:T(8,128)} %param.9) | data formatting | bytes 65536 | tf_op args[3]
  2.2 114.4 %log_linear.1 = (bf16[1,512,1024]{2,1,0:T(8,128)(2,1)}, bf16[1,512,512]{2,1,0:T(8,128)(2,1)}, bf16[1,512,512]{2,1,0:T(8,128)(2,1)}, bf16[1,512,512]{2,1,0:T(8,128)(2,1)}) custom-call(bf16[1,512,512]{2,1,0:T(8,128)(2,1)} %q_hbm.1, bf16[1,512,512]{2,1,0:T(8,128)(2,1)} %k_hbm.1, bf16[1,512,512]{2,1,0:T(8,128)(2,1)} %v_hbm.1, s32[1,512,16]{2,1,0:T(8,128)} %copy.10.m_hbm, ...), custom_call_target="tpu_custom_call" | custom-call | tf_op jit(solution)/shard_map/log_linear/pallas_call | solution.py:509
  116.6 0.0 copy-start.2
  116.7 0.0 copy-start.1
  116.7 0.0 copy-start
  116.7 2.4 %copy.15 = bf16[1,512,1024]{2,1,0:T(8,128)(2,1)} copy(bf16[1,512,1024]{2,1,0:T(8,128)(2,1)} %get-tuple-element.8) | data formatting | bytes 2097152
  119.1 0.0 copy-done.2
  119.1 0.8 copy.16
  119.8 0.0 copy-done.1
  119.9 0.8 copy.17
  120.6 0.0 copy-done
  120.6 0.8 copy.18
Async XLA Ops:
  116.6 2.4 %copy-start.2 = (bf16[1,512,512]{2,1,0:T(8,128)(2,1)S(1)}, bf16[1,512,512]{2,1,0:T(8,128)(2,1)}, u32[]{:S(2)}) copy-start(bf16[1,512,512]{2,1,0:T(8,128)(2,1)} %get-tuple-element.9) | copy-start | bytes 1572868
  116.7 3.2 %copy-start.1 = (bf16[1,512,512]{2,1,0:T(8,128)(2,1)S(1)}, bf16[1,512,512]{2,1,0:T(8,128)(2,1)}, u32[]{:S(2)}) copy-start(bf16[1,512,512]{2,1,0:T(8,128)(2,1)} %get-tuple-element.10) | copy-start | bytes 1572868
  116.7 4.0 %copy-start = (bf16[1,512,512]{2,1,0:T(8,128)(2,1)S(1)}, bf16[1,512,512]{2,1,0:T(8,128)(2,1)}, u32[]{:S(2)}) copy-start(bf16[1,512,512]{2,1,0:T(8,128)(2,1)} %get-tuple-element.11) | copy-start | bytes 1572868

commit v2 on v1

--- a/solution.py
+++ b/solution.py
@@ -35,10 +35,10 @@
     n_seq, heads, length, half_d,
     q_hbm, k_hbm, v_hbm, m_hbm, w_hbm, go_hbm,
     lay_hbm, gq_hbm, gk_hbm, gv_hbm,
-    qv, kv, vv, mv, wv, go, gop, wp,
+    qv, kv, vv, mt, mv, wv, go, gop, wp,
     blend, mb, gacc, gm, state, fr, agg, reach, out, br, total,
-    lo, ql, kl, vl, mix, mixp, lay, gq, gk, gv,
-    in_sem, out_sem, hs_send, hs_recv, mx_send, mx_recv, fs, fr_sem, bs, br_sem,
+    lo, ql, kl, vl, mix, mixp, lay, gq, gk, gv, ur, qt,
+    in_sem, out_sem, hs_send, hs_recv, mx_send, mx_recv, fs, fr_sem, bs, br_sem, us, ur_sem, ready,
 ):
     n = lax.axis_index("seq")
     core = lax.axis_index("head")
@@ -49,43 +49,43 @@
     r = lax.rem(n, 4)
     up = [lax.rem(n >> j, 2) for j in range(span)]
     nxt = [lax.rem((n + 1) >> j, 2) for j in range(span)]
-    last = n == n_seq - 1
+    top_level = span - 1
+    n_half = n_seq // 2
+    upper = up[top_level] == 1
+    inner = lax.rem(n, n_half)
+    after = [lax.rem((inner + 1) >> j, 2) for j in range(top_level)]
+    last = inner == n_half - 1
+    end = n == n_seq - 1
     pending = []
+    slots = m_hbm.shape[1]
 
     barrier = pltpu.get_barrier_semaphore()
-    dists = (1, n_seq - 1, 2, n_seq - 2, 4, n_seq - 4)
+    dists = (1, 2, 4)
     pl.semaphore_signal(barrier, inc=1, device_id={"head": other}, device_id_type=MESH)
     for d in dists:
-        pl.semaphore_signal(
-            barrier, inc=1, device_id={"seq": lax.rem(n + d, n_seq)}, device_id_type=MESH
-        )
+
+        @pl.when(n + d < n_seq)
+        def _():
+            pl.semaphore_signal(barrier, inc=1, device_id={"seq": n + d}, device_id_type=MESH)
+
+    for first in (0, 3):
+
+        @pl.when(n == first)
+        def _():
+            pl.semaphore_signal(barrier, inc=1, device_id={"seq": n_seq - 1}, device_id_type=MESH)
 
     loads = [
         pltpu.make_async_copy(src, dst, in_sem.at[i])
         for i, (src, dst) in enumerate(
             ((k_hbm.at[0], kv), (v_hbm.at[0], vv), (go_hbm.at[0], go), (w_hbm, wv),
-             (m_hbm.at[0], mv), (q_hbm.at[0], qv))
+             (m_hbm.at[0], mt.at[pl.ds(0, slots)]), (q_hbm.at[0], qv))
         )
     ]
-    for load in loads:
-        load.start()
-    loads[0].wait()
-    loads[1].wait()
-
-    def cols(h):
-        return pl.ds(pl.multiple_of(h * HD, HD), HD)
-
-    def state_body(h, carry):
-        s = tn(kv[:, cols(h)], vv[:, cols(h)])
-        state[h] = s
-        agg[h] = s.astype(BF16)
-        return carry
-
-    lax.fori_loop(0, heads, state_body, 0)
-    loads[2].wait()
-    loads[3].wait()
-
-    pl.semaphore_wait(barrier, 1 + len(dists))
+    for i in (5, 4, 2, 3, 0, 1):
+        loads[i].start()
+
+    one = lambda cond: cond.astype(jnp.int32)
+    pl.semaphore_wait(barrier, 1 + one(n >= 1) + one(n >= 2) + one(n >= 4) + 2 * one(end))
 
     own_cols = pl.ds(pl.multiple_of(core * half_d, HD), half_d)
     other_cols = pl.ds(pl.multiple_of(other * half_d, HD), half_d)
@@ -96,9 +96,44 @@
             device_id={"head": other}, device_id_type=MESH,
         )
 
-    go_copy = to_core(go, gop, 0)
-    w_copy = to_core(wv.at[:, other_cols], wp, 1)
+    go_copy = to_core(go_hbm.at[0], gop, 0)
+    w_copy = to_core(w_hbm.at[:, other_cols], wp, 1)
     go_copy.start()
+    w_copy.start()
+    for d in dists:
+
+        @pl.when(n >= d)
+        def _():
+            pl.semaphore_signal(ready, inc=1, device_id={"seq": n - d}, device_id_type=MESH)
+
+    def cols(h):
+        return pl.ds(pl.multiple_of(h * HD, HD), HD)
+
+    loads[5].wait()
+    loads[4].wait()
+    mt[slots:, :] = jnp.zeros((HD - slots, length), jnp.int32)
+    mv[...] = mt[...].astype(F32).T
+    for j in range(span):
+        mb[j] = jnp.broadcast_to(mv[:, tiers + j : tiers + j + 1], (length, HD)).astype(BF16)
+
+    def turn_body(h, carry):
+        q = qv[:, cols(h)].astype(F32)
+        qt[0, h] = q.T.astype(BF16)
+        qt[1, h] = (q * ROOT_HALF).T.astype(BF16)
+        return carry
+
+    lax.fori_loop(0, heads, turn_body, 0)
+
+    def gm_body(i, carry):
+        rows = pl.ds(pl.multiple_of(lax.rem(i, 2) * half, half), half)
+        wide = heads * HD // 2
+        feats = pl.ds(pl.multiple_of(i // 2 * wide, wide), wide)
+        gacc[rows, feats] = nt(go[rows, :], wv[feats, own_cols])
+        return carry
+
+    loads[2].wait()
+    loads[3].wait()
+    lax.fori_loop(0, 4, gm_body, 0)
 
     def fmsg(level, which, c, src, dist):
         return pltpu.make_async_remote_copy(
@@ -126,87 +161,127 @@
     def bwait(level, slot, c):
         bmsg(level, slot, c, 0).wait_recv()
 
+    def umsg(which, slot, c, dist, src=None):
+        return pltpu.make_async_remote_copy(
+            src_ref=out.at[top_level, c] if src is None else src, dst_ref=ur.at[slot, c],
+            send_sem=us.at[which, c], recv_sem=ur_sem.at[slot, c],
+            device_id={"seq": lax.rem(n + dist, n_seq)}, device_id_type=MESH,
+        )
+
+    def uwait(slot, c):
+        umsg(0, slot, c, 0).wait_recv()
+
     even = lax.rem(r, 2) == 0
 
-    @pl.when(even)
-    def _():
-        for c in range(heads):
-            fsend(0, 1, c, agg.at[c], 1)
-
-    w_copy.start()
-
-    def gm_body(source, weight_cols, finish):
-        def body(i, carry):
-            rows = pl.ds(pl.multiple_of(lax.rem(i, 2) * half, half), half)
-            wide = heads * HD // 2
-            feats = pl.ds(pl.multiple_of(i // 2 * wide, wide), wide)
-            part = nt(source[rows, :], wv[feats, weight_cols])
-            if finish:
-                gm[rows, feats] = (gacc[rows, feats] + part).astype(BF16)
-            else:
-                gacc[rows, feats] = part
-            return carry
-
-        lax.fori_loop(0, 4, body, 0)
-
-    gm_body(go, own_cols, False)
-
-    @pl.when(r == 1)
-    def _():
-        for c in range(heads):
-            fwait(0, c)
-            agg[c] = (state[c] + fr[0, c].astype(F32)).astype(BF16)
-            fsend(1, 0, c, agg.at[c], 2)
-            fsend(1, 1, c, agg.at[c], 1)
-
-    @pl.when(r == 3)
-    def _():
-        for c in range(heads):
-            fwait(0, c)
-            state[c] = state[c] + fr[0, c].astype(F32)
-
-    loads[4].wait()
-    loads[5].wait()
-
-    for j in range(span):
-        mb[j] = jnp.broadcast_to(mv[:, tiers + j : tiers + j + 1].astype(F32), (length, HD)).astype(BF16)
-
-    go_copy.wait_recv()
-    gm_body(gop, other_cols, True)
-
-    def source_of(level):
-        return jnp.logical_and(nxt[level] == 1, up[level] == 0)
-
-    @pl.when(r == 3)
-    def _():
-        first = source_of(2)
-        for c in range(heads):
-            fwait(1, c)
-            tot = state[c] + fr[1, c].astype(F32)
-            state[c] = tot
-            agg[c] = tot.astype(BF16)
-
-            @pl.when(first)
-            def _():
-                fsend(2, 0, c, agg.at[c], 4)
-                fsend(2, 1, c, agg.at[c], 1)
+    def state_body(h, carry):
+        s = tn(kv[:, cols(h)], vv[:, cols(h)])
+        state[h] = s
+        agg[h] = s.astype(BF16)
+        return carry
+
+    def upper_in():
+        @pl.when(jnp.logical_not(end))
+        def _():
+            pl.semaphore_wait(
+                ready, one(n + 1 < n_seq) + one(n + 2 < n_seq) + one(n + 4 < n_seq)
+            )
+
+    def open_forward():
+        lax.fori_loop(0, heads, state_body, 0)
+
+        @pl.when(jnp.logical_not(upper))
+        def _():
+            upper_in()
+
+        @pl.when(even)
+        def _():
+            for c in range(heads):
+                fsend(0, 1, c, agg.at[c], 1)
+
+    loads[0].wait()
+    loads[1].wait()
+
+    @pl.when(n == 0)
+    def _():
+        open_forward()
 
     def halves(j):
         odd = (tiers + j - 1) % 2
         return odd, 2.0 ** (-((tiers + j - 1 - odd) // 2))
 
+    def reach_level(j, h, g):
+        odd, whole = halves(j)
+        s = nn(qt[odd, h], mb[j] * g) * whole
+        reach[j, h] = s
+        out[j, h] = s.astype(BF16)
+
+    @pl.when(upper)
+    def _():
+        upper_in()
+
+    go_copy.wait_recv()
+
+    def finish_body(h, carry):
+        g = (gacc[:, cols(h)] + nt(gop[...], wv[cols(h), other_cols])).astype(BF16)
+        gm[:, cols(h)] = g
+
+        @pl.when(upper)
+        def _():
+            reach_level(top_level, h, g)
+
+            @pl.when(r == 0)
+            def _():
+                umsg(0, 0, h, 1).start()
+
+            @pl.when(r == 2)
+            def _():
+                umsg(0, 1, h, 1).start()
+
+        return carry
+
+    lax.fori_loop(0, heads, finish_body, 0)
+
+    def joined(c, slots_in):
+        tot = reach[top_level, c]
+        for slot in slots_in:
+            uwait(slot, c)
+            tot = tot + ur[slot, c].astype(F32)
+        return tot
+
+    @pl.when(jnp.logical_and(upper, r == 1))
+    def _():
+        for c in range(heads):
+            out[top_level, c] = joined(c, (0,)).astype(BF16)
+            umsg(0, 0, c, 2).start()
+
+    @pl.when(jnp.logical_and(upper, r == 3))
+    def _():
+        @pl.when(inner == 3)
+        def _():
+            for c in range(heads):
+                out[top_level, c] = joined(c, (0, 1)).astype(BF16)
+                umsg(0, 2, c, 4).start()
+
+        @pl.when(jnp.logical_and(inner != 3, jnp.logical_not(end)))
+        def _():
+            for c in range(heads):
+                out[top_level, c] = joined(c, (0, 1, 2)).astype(BF16)
+                umsg(0, 2, c, 4).start()
+
+        @pl.when(end)
+        def _():
+            for c in range(heads):
+                out[top_level, c] = joined(c, (0, 1, 2)).astype(BF16)
+                umsg(1, 3, c, 1).start()
+                umsg(0, 3, c, 4).start()
+
     def reach_body(h, carry):
-        q = qv[:, cols(h)]
-        qs = (q.astype(F32) * ROOT_HALF).astype(BF16)
         g = gm[:, cols(h)]
-        for j in range(span):
-            odd, whole = halves(j)
+        for j in range(top_level):
 
             @pl.when(up[j] == 1)
             def _():
-                s = tn(qs if odd else q, mb[j] * g) * whole
-                reach[j, h] = s
-                out[j, h] = s.astype(BF16)
+                reach_level(j, h, g)
 
         return carry
 
@@ -215,7 +290,7 @@
     def bsent(cond, level):
         pending.append((cond, lambda: [bmsg(level, 0, c, 0).wait_send() for c in range(heads)]))
 
-    high = list(range(span - 1, 1, -1))
+    high = list(range(top_level - 1, 1, -1))
     for j in high:
 
         @pl.when(jnp.logical_and(r == 2, up[j] == 1))
@@ -240,8 +315,28 @@
         for c in range(heads):
             bmsg(0, 0, c, 1).start()
 
-    for j in range(span):
-        bsent(up[j] == 1, j)
+    for j in range(top_level):
+        early = False
+        if 1 <= j < top_level - 1:
+            early = jnp.logical_and(jnp.logical_and(r == 3, after[j + 1] == 1), up[j + 1] == 0)
+        bsent(jnp.logical_and(up[j] == 1, jnp.logical_not(early)), j)
+
+    def chain_step(j, position, slot):
+        @pl.when(jnp.logical_and(up[j] == 1, r == position))
+        def _():
+            for c in range(heads):
+                bwait(j, 2, c)
+                out[j, c] = (reach[j, c] + br[j, 2, c].astype(F32)).astype(BF16)
+                bmsg(j, slot, c, 1).start()
+
+    @pl.when(n != 0)
+    def _():
+        open_forward()
+
+    for j in high:
+        chain_step(j, 1, 2)
+    for j in high:
+        chain_step(j, 0, 0)
 
     def blend_block(rows, levels):
         t = lax.broadcasted_iota(jnp.int32, (half, half), 0)
@@ -249,7 +344,7 @@
         spread = jnp.bitwise_xor(t, s)
 
         def column(level):
-            return mv[rows, level : level + 1].astype(F32) * tier_scale(level)
+            return mv[rows, level : level + 1] * tier_scale(level)
 
         value = jnp.broadcast_to(column(0), (half, half))
         for level in range(1, levels):
@@ -260,7 +355,7 @@
     blend[0] = blend_block(top, tiers - 1)
     blend[1] = blend_block(low, tiers - 1)
     blend[2] = jnp.broadcast_to(
-        mv[low, tiers - 1 : tiers].astype(F32) * tier_scale(tiers - 1), (half, half)
+        mv[low, tiers - 1 : tiers] * tier_scale(tiers - 1), (half, half)
     )
 
     def forward_step(j):
@@ -296,19 +391,11 @@
         def _():
             forward_step(j)
 
-    def chain_step(j, position, slot):
-        @pl.when(jnp.logical_and(up[j] == 1, r == position))
-        def _():
-            for c in range(heads):
-                bwait(j, 2, c)
-                out[j, c] = (reach[j, c] + br[j, 2, c].astype(F32)).astype(BF16)
-                bmsg(j, slot, c, 1).start()
-
     def down(level):
         return {0: (0, 1), 1: (1, 2)}.get(level, (1, 4))
 
     def back_step(j):
-        @pl.when(jnp.logical_and(r == 3, nxt[j] == 1))
+        @pl.when(jnp.logical_and(r == 3, after[j] == 1))
         def _():
             @pl.when(up[j] == 1)
             def _():
@@ -329,6 +416,8 @@
                     out[j - 1, c] = (reach[j - 1, c] + tot).astype(BF16)
                     slot, dist = down(j - 1)
                     bmsg(j - 1, slot, c, dist).start()
+                for c in range(heads):
+                    bmsg(j - 1, slot, c, dist).wait_send()
                 for level in range(j - 2, -1, -1):
                     slot, dist = down(level)
                     for c in range(heads):
@@ -362,26 +451,40 @@
 
     def local_body(i, carry):
         local_head(i)
-
-        @pl.when(i == 0)
-        def _():
-            when_forward(2, busy)
-            for j in high:
-                chain_step(j, 1, 2)
-            for j in high:
-                chain_step(j, 0, 0)
-
-        @pl.when(i == 2)
-        def _():
-            for j in range(3, span - 1):
-                when_forward(j, busy)
-
         return carry
 
     lax.fori_loop(0, heads, local_body, 0)
+
+    @pl.when(r == 1)
+    def _():
+        for c in range(heads):
+            fwait(0, c)
+            agg[c] = (state[c] + fr[0, c].astype(F32)).astype(BF16)
+            fsend(1, 0, c, agg.at[c], 2)
+            fsend(1, 1, c, agg.at[c], 1)
+
+    def source_of(level):
+        return jnp.logical_and(nxt[level] == 1, up[level] == 0)
+
+    @pl.when(r == 3)
+    def _():
+        first = source_of(2)
+        for c in range(heads):
+            fwait(0, c)
+            state[c] = state[c] + fr[0, c].astype(F32)
+        for c in range(heads):
+            fwait(1, c)
+            tot = state[c] + fr[1, c].astype(F32)
+            state[c] = tot
+            agg[c] = tot.astype(BF16)
+
+            @pl.when(first)
+            def _():
+                fsend(2, 0, c, agg.at[c], 4)
+                fsend(2, 1, c, agg.at[c], 1)
+
     for j in high:
         back_step(j)
-    when_forward(span - 1, busy)
 
     @pl.when(r == 1)
     def _():
@@ -392,6 +495,11 @@
             total[c] = tot
             out[0, c] = (reach[0, c] + tot).astype(BF16)
             bmsg(0, 0, c, 1).start()
+
+    when_forward(2, busy)
+    for j in range(3, top_level):
+        when_forward(j, busy)
+    when_forward(top_level, busy)
 
     @pl.when(r == 2)
     def _():
@@ -466,6 +574,20 @@
         total[...] = jnp.zeros(total.shape, F32)
 
     def back_body(h, carry):
+        @pl.when(jnp.logical_not(upper))
+        def _():
+            uwait(3, h)
+
+            @pl.when(jnp.logical_and(r == 3, jnp.logical_not(last)))
+            def _():
+                umsg(0, 3, h, 4, ur.at[3, h]).start()
+
+            @pl.when(jnp.logical_or(r < 2, jnp.logical_and(r == 3, jnp.logical_not(last))))
+            def _():
+                umsg(1, 3, h, 1, ur.at[3, h]).start()
+
+            total[h] = total[h] + ur[3, h].astype(F32)
+
         back = total[h].astype(BF16)
         gk[:, cols(h)] = (kl[:, cols(h)] + nt(vv[:, cols(h)], back)).astype(BF16)
         gv[:, cols(h)] = (vl[:, cols(h)] + nn(kv[:, cols(h)], back)).astype(BF16)
@@ -482,6 +604,14 @@
         sends = jnp.logical_and(r == 3, nxt[j] == 1)
         fsent(sends, j, 0)
         fsent(jnp.logical_or(sends, jnp.logical_and(r < 2, up[j] == 1)), j, 1)
+
+    def usent(cond, which):
+        pending.append((cond, lambda: [umsg(which, 3, c, 0).wait_send() for c in range(heads)]))
+
+    lower_hop = jnp.logical_and(jnp.logical_not(upper), jnp.logical_and(r == 3, jnp.logical_not(last)))
+    usent(jnp.logical_or(upper, lower_hop), 0)
+    lower_near = jnp.logical_or(lower_hop, jnp.logical_and(jnp.logical_not(upper), r < 2))
+    usent(jnp.logical_or(end, lower_near), 1)
     for cond, wait in pending:
 
         @pl.when(cond)
@@ -518,7 +648,8 @@
         out_specs=(any_spec,) * 4,
         scratch_shapes=[
             wide(BF16), wide(BF16), wide(BF16),
-            pltpu.VMEM(level_mask.shape[1:], jnp.int32),
+            pltpu.VMEM((HD, length), jnp.int32),
+            pltpu.VMEM((length, HD), F32),
             pltpu.VMEM(out_weight.shape, BF16),
             pltpu.VMEM((length, half_d), BF16),
             pltpu.VMEM((length, half_d), BF16),
@@ -537,12 +668,15 @@
             wide(BF16), wide(BF16),
             pltpu.VMEM((length, half_d), BF16),
             wide(BF16), wide(BF16), wide(BF16),
+            pltpu.VMEM((4, heads, HD, HD), BF16),
+            pltpu.VMEM((2, heads, HD, length), BF16),
             dma(6), dma(4), dma(2), dma(2), dma(heads), dma(heads),
             dma(span, 2, heads), dma(span, heads), dma(span, heads), dma(span, 3, heads),
+            dma(2, heads), dma(4, heads), pltpu.SemaphoreType.REGULAR,
         ],
         compiler_params=pltpu.CompilerParams(collective_id=0, has_side_effects=True),
         name="log_linear",
-    )(query_in, key_in, value_in, level_mask, out_weight, grad_out)
+    )(query_in, key_in, value_in, jnp.swapaxes(level_mask, 1, 2), out_weight, grad_out)
     return layer, gq, gk, gv
 
 

time: 122 us -> 87.6 us (0.72)
  the two profiles are of different devices: /device:TPU:97 before, /device:TPU:160 now
where the time goes in v2:
time: 87.6 us; the launch traced here: 87.4 us
  Pallas kernels  82 us (94%)
  local copies, waits for them, and re-layouts  4.77 us (5%)
    pallas_call x1, Pallas kernels, on_device(): pl.pallas_call(functools.partial(kernel, n_seq, heads, length, half_d), o...  82 us
    unnamed x10, local copies, waits for them, and re-layouts  4.77 us

profile of v2, /device:TPU:160, one launch (start us, length us, event | category | flops | bytes accessed | tf_op | source)
XLA Modules:
  0.0 87.4 jit_solution(1757148837968133168)
XLA Ops:
  0.6 82.0 %log_linear.1 = (bf16[1,512,1024]{2,1,0:T(8,128)(2,1)}, bf16[1,512,512]{2,1,0:T(8,128)(2,1)}, bf16[1,512,512]{2,1,0:T(8,128)(2,1)}, bf16[1,512,512]{2,1,0:T(8,128)(2,1)}) custom-call(bf16[1,512,512]{2,1,0:T(8,128)(2,1)} %q_hbm.1, bf16[1,512,512]{2,1,0:T(8,128)(2,1)} %k_hbm.1, bf16[1,512,512]{2,1,0:T(8,128)(2,1)} %v_hbm.1, s32[1,16,512]{2,1,0:T(8,128)} %bitcast.1, ...), custom_call_target="tpu_custom_call" | custom-call | tf_op jit(solution)/shard_map/log_linear/pallas_call | solution.py:639
  82.6 0.0 copy-start.2
  82.7 0.0 copy-start.1
  82.7 0.0 copy-start
  82.7 2.4 %copy.14 = bf16[1,512,1024]{2,1,0:T(8,128)(2,1)} copy(bf16[1,512,1024]{2,1,0:T(8,128)(2,1)} %get-tuple-element.8) | data formatting | bytes 2097152
  85.1 0.0 copy-done.2
  85.1 0.8 copy.15
  85.8 0.0 copy-done.1
  85.9 0.8 copy.16
  86.6 0.0 copy-done
  86.6 0.8 copy.17
Async XLA Ops:
  82.6 2.4 %copy-start.2 = (bf16[1,512,512]{2,1,0:T(8,128)(2,1)S(1)}, bf16[1,512,512]{2,1,0:T(8,128)(2,1)}, u32[]{:S(2)}) copy-start(bf16[1,512,512]{2,1,0:T(8,128)(2,1)} %get-tuple-element.9) | copy-start | bytes 1572868
  82.7 3.2 %copy-start.1 = (bf16[1,512,512]{2,1,0:T(8,128)(2,1)S(1)}, bf16[1,512,512]{2,1,0:T(8,128)(2,1)}, u32[]{:S(2)}) copy-start(bf16[1,512,512]{2,1,0:T(8,128)(2,1)} %get-tuple-element.10) | copy-start | bytes 1572868
  82.7 4.0 %copy-start = (bf16[1,512,512]{2,1,0:T(8,128)(2,1)S(1)}, bf16[1,512,512]{2,1,0:T(8,128)(2,1)}, u32[]{:S(2)}) copy-start(bf16[1,512,512]{2,1,0:T(8,128)(2,1)} %get-tuple-element.11) | copy-start | bytes 1572868

commit v3 on v2

--- a/solution.py
+++ b/solution.py
@@ -68,6 +68,11 @@
         def _():
             pl.semaphore_signal(barrier, inc=1, device_id={"seq": n + d}, device_id_type=MESH)
 
+    @pl.when(inner == 7)
+    def _():
+        for d in (7, 8):
+            pl.semaphore_signal(barrier, inc=1, device_id={"seq": n + d}, device_id_type=MESH)
+
     for first in (0, 3):
 
         @pl.when(n == first)
@@ -85,7 +90,7 @@
         loads[i].start()
 
     one = lambda cond: cond.astype(jnp.int32)
-    pl.semaphore_wait(barrier, 1 + one(n >= 1) + one(n >= 2) + one(n >= 4) + 2 * one(end))
+    pl.semaphore_wait(barrier, 1 + one(n >= 1) + one(n >= 2) + one(n >= 4) + 2 * one(end) + one(inner >= 14))
 
     own_cols = pl.ds(pl.multiple_of(core * half_d, HD), half_d)
     other_cols = pl.ds(pl.multiple_of(other * half_d, HD), half_d)
@@ -100,11 +105,15 @@
     w_copy = to_core(w_hbm.at[:, other_cols], wp, 1)
     go_copy.start()
     w_copy.start()
-    for d in dists:
+    for i, d in enumerate(dists):
 
         @pl.when(n >= d)
         def _():
-            pl.semaphore_signal(ready, inc=1, device_id={"seq": n - d}, device_id_type=MESH)
+            pl.semaphore_signal(ready.at[i], inc=1, device_id={"seq": n - d}, device_id_type=MESH)
+
+    @pl.when(end)
+    def _():
+        pl.semaphore_signal(ready.at[3], inc=1, device_id={"seq": n - 8}, device_id_type=MESH)
 
     def cols(h):
         return pl.ds(pl.multiple_of(h * HD, HD), HD)
@@ -179,19 +188,21 @@
         agg[h] = s.astype(BF16)
         return carry
 
-    def upper_in():
-        @pl.when(jnp.logical_not(end))
-        def _():
-            pl.semaphore_wait(
-                ready, one(n + 1 < n_seq) + one(n + 2 < n_seq) + one(n + 4 < n_seq)
-            )
+    soon = (
+        jnp.logical_or(upper, r < 2),
+        jnp.logical_and(upper, r == 1),
+        jnp.logical_and(upper, r == 3),
+    )
+
+    def upper_in(i, cond):
+        @pl.when(jnp.logical_and(cond, n + dists[i] < n_seq))
+        def _():
+            pl.semaphore_wait(ready.at[i], 1)
 
     def open_forward():
         lax.fori_loop(0, heads, state_body, 0)
-
-        @pl.when(jnp.logical_not(upper))
-        def _():
-            upper_in()
+        for i in range(3):
+            upper_in(i, jnp.logical_not(soon[i]))
 
         @pl.when(even)
         def _():
@@ -200,6 +211,8 @@
 
     loads[0].wait()
     loads[1].wait()
+
+    upper_in(0, soon[0])
 
     @pl.when(n == 0)
     def _():
@@ -215,10 +228,6 @@
         reach[j, h] = s
         out[j, h] = s.astype(BF16)
 
-    @pl.when(upper)
-    def _():
-        upper_in()
-
     go_copy.wait_recv()
 
     def finish_body(h, carry):
@@ -240,6 +249,9 @@
         return carry
 
     lax.fori_loop(0, heads, finish_body, 0)
+
+    for i in (1, 2):
+        upper_in(i, soon[i])
 
     def joined(c, slots_in):
         tot = reach[top_level, c]
@@ -259,25 +271,67 @@
         @pl.when(inner == 3)
         def _():
             for c in range(heads):
-                out[top_level, c] = joined(c, (0, 1)).astype(BF16)
+                out[top_level, c] = joined(c, (1, 0)).astype(BF16)
                 umsg(0, 2, c, 4).start()
 
-        @pl.when(jnp.logical_and(inner != 3, jnp.logical_not(end)))
-        def _():
-            for c in range(heads):
-                out[top_level, c] = joined(c, (0, 1, 2)).astype(BF16)
+        @pl.when(inner == 7)
+        def _():
+            pl.semaphore_wait(ready.at[3], 1)
+            for c in range(heads):
+                out[top_level, c] = joined(c, (1, 0, 2)).astype(BF16)
+                umsg(0, 3, c, 8).start()
+
+        @pl.when(inner == 11)
+        def _():
+            for c in range(heads):
+                out[top_level, c] = joined(c, (1, 0)).astype(BF16)
                 umsg(0, 2, c, 4).start()
 
         @pl.when(end)
         def _():
             for c in range(heads):
-                out[top_level, c] = joined(c, (0, 1, 2)).astype(BF16)
+                out[top_level, c] = joined(c, (1, 0, 2, 3)).astype(BF16)
                 umsg(1, 3, c, 1).start()
                 umsg(0, 3, c, 4).start()
 
+    next_level = top_level - 1
+
+    def next_body(h, carry):
+        @pl.when(up[next_level] == 1)
+        def _():
+            reach_level(next_level, h, gm[:, cols(h)])
+
+            @pl.when(r == 0)
+            def _():
+                bmsg(next_level, 2, h, -1).start()
+
+            @pl.when(inner == 11)
+            def _():
+                bmsg(next_level, 1, h, 4).start()
+
+            @pl.when(last)
+            def _():
+                bmsg(next_level, 3, h, 8).start()
+
+        return carry
+
+    lax.fori_loop(0, heads, next_body, 0)
+
+    def chain_step(j, where, slot, dist):
+        @pl.when(jnp.logical_and(up[j] == 1, where))
+        def _():
+            for c in range(heads):
+                bwait(j, 2, c)
+                out[j, c] = (reach[j, c] + br[j, 2, c].astype(F32)).astype(BF16)
+                bmsg(j, slot, c, dist).start()
+
+    chain_step(next_level, r == 1, 2, -1)
+    chain_step(next_level, inner == 10, 0, 3)
+    chain_step(next_level, inner == 14, 2, 7)
+
     def reach_body(h, carry):
         g = gm[:, cols(h)]
-        for j in range(top_level):
+        for j in range(next_level):
 
             @pl.when(up[j] == 1)
             def _():
@@ -287,56 +341,9 @@
 
     lax.fori_loop(0, heads, reach_body, 0)
 
-    def bsent(cond, level):
-        pending.append((cond, lambda: [bmsg(level, 0, c, 0).wait_send() for c in range(heads)]))
-
-    high = list(range(top_level - 1, 1, -1))
-    for j in high:
-
-        @pl.when(jnp.logical_and(r == 2, up[j] == 1))
-        def _():
-            for c in range(heads):
-                bmsg(j, 2, c, 1).start()
-
-        @pl.when(last)
-        def _():
-            for c in range(heads):
-                bmsg(j, 1, c, 4).start()
-
-    @pl.when(r == 2)
-    def _():
-        for c in range(heads):
-            bmsg(1, 0, c, 1).start()
-
-    @pl.when(last)
-    def _():
-        for c in range(heads):
-            bmsg(1, 1, c, 2).start()
-        for c in range(heads):
-            bmsg(0, 0, c, 1).start()
-
-    for j in range(top_level):
-        early = False
-        if 1 <= j < top_level - 1:
-            early = jnp.logical_and(jnp.logical_and(r == 3, after[j + 1] == 1), up[j + 1] == 0)
-        bsent(jnp.logical_and(up[j] == 1, jnp.logical_not(early)), j)
-
-    def chain_step(j, position, slot):
-        @pl.when(jnp.logical_and(up[j] == 1, r == position))
-        def _():
-            for c in range(heads):
-                bwait(j, 2, c)
-                out[j, c] = (reach[j, c] + br[j, 2, c].astype(F32)).astype(BF16)
-                bmsg(j, slot, c, 1).start()
-
     @pl.when(n != 0)
     def _():
         open_forward()
-
-    for j in high:
-        chain_step(j, 1, 2)
-    for j in high:
-        chain_step(j, 0, 0)
 
     def blend_block(rows, levels):
         t = lax.broadcasted_iota(jnp.int32, (half, half), 0)
@@ -395,34 +402,24 @@
         return {0: (0, 1), 1: (1, 2)}.get(level, (1, 4))
 
     def back_step(j):
-        @pl.when(jnp.logical_and(r == 3, after[j] == 1))
-        def _():
-            @pl.when(up[j] == 1)
-            def _():
+        @pl.when(jnp.logical_and(jnp.logical_and(r == 3, after[j] == 1), up[j] == 0))
+        def _():
+            slot, dist = down(j - 1)
+            for c in range(heads):
+                tot = jnp.zeros((HD, HD), F32)
+                for source in range(4 if j == next_level else 2):
+                    bwait(j, source, c)
+                    tot = tot + br[j, source, c].astype(F32)
+                total[c] = tot
+                out[j - 1, c] = (reach[j - 1, c] + tot).astype(BF16)
+                bmsg(j - 1, slot, c, dist).start()
+            for c in range(heads):
+                bmsg(j - 1, slot, c, dist).wait_send()
+            for level in range(j - 2, -1, -1):
+                slot, dist = down(level)
                 for c in range(heads):
-                    bwait(j, 0, c)
-                    bwait(j, 1, c)
-                    tot = br[j, 0, c].astype(F32) + br[j, 1, c].astype(F32)
-                    out[j, c] = (reach[j, c] + tot).astype(BF16)
-                    bmsg(j, 1, c, 4).start()
-
-            @pl.when(up[j] == 0)
-            def _():
-                for c in range(heads):
-                    bwait(j, 0, c)
-                    bwait(j, 1, c)
-                    tot = br[j, 0, c].astype(F32) + br[j, 1, c].astype(F32)
-                    total[c] = tot
-                    out[j - 1, c] = (reach[j - 1, c] + tot).astype(BF16)
-                    slot, dist = down(j - 1)
-                    bmsg(j - 1, slot, c, dist).start()
-                for c in range(heads):
-                    bmsg(j - 1, slot, c, dist).wait_send()
-                for level in range(j - 2, -1, -1):
-                    slot, dist = down(level)
-                    for c in range(heads):
-                        out[level, c] = (reach[level, c] + total[c]).astype(BF16)
-                        bmsg(level, slot, c, dist).start()
+                    out[level, c] = (reach[level, c] + total[c]).astype(BF16)
+                    bmsg(level, slot, c, dist).start()
 
     def local_head(h):
         def parts(ref):
@@ -455,6 +452,34 @@
 
     lax.fori_loop(0, heads, local_body, 0)
 
+    def bsent(cond, level):
+        pending.append((cond, lambda: [bmsg(level, 0, c, 0).wait_send() for c in range(heads)]))
+
+    @pl.when(jnp.logical_and(r == 0, up[2] == 1))
+    def _():
+        for c in range(heads):
+            bmsg(2, 2, c, -1).start()
+
+    @pl.when(r == 2)
+    def _():
+        for c in range(heads):
+            bmsg(1, 0, c, 1).start()
+
+    @pl.when(last)
+    def _():
+        for level, slot, dist in ((2, 1, 4), (1, 1, 2), (0, 0, 1)):
+            for c in range(heads):
+                bmsg(level, slot, c, dist).start()
+
+    for j in range(top_level):
+        early = False
+        if 1 <= j < next_level:
+            early = jnp.logical_and(jnp.logical_and(r == 3, after[j + 1] == 1), up[j + 1] == 0)
+        bsent(jnp.logical_and(up[j] == 1, jnp.logical_not(early)), j)
+
+    chain_step(2, r == 1, 2, -1)
+    chain_step(2, r == 2, 0, 3)
+
     @pl.when(r == 1)
     def _():
         for c in range(heads):
@@ -483,7 +508,7 @@
                 fsend(2, 0, c, agg.at[c], 4)
                 fsend(2, 1, c, agg.at[c], 1)
 
-    for j in high:
+    for j in (3, 2):
         back_step(j)
 
     @pl.when(r == 1)
@@ -662,7 +687,7 @@
             pltpu.VMEM((heads, HD, HD), BF16),
             pltpu.VMEM((span, heads, HD, HD), F32),
             pltpu.VMEM((span, heads, HD, HD), BF16),
-            pltpu.VMEM((span, 3, heads, HD, HD), BF16),
+            pltpu.VMEM((span, 4, heads, HD, HD), BF16),
             pltpu.VMEM((heads, HD, HD), F32),
             wide(F32), wide(F32), wide(F32), wide(F32),
             wide(BF16), wide(BF16),
@@ -671,8 +696,8 @@
             pltpu.VMEM((4, heads, HD, HD), BF16),
             pltpu.VMEM((2, heads, HD, length), BF16),
             dma(6), dma(4), dma(2), dma(2), dma(heads), dma(heads),
-            dma(span, 2, heads), dma(span, heads), dma(span, heads), dma(span, 3, heads),
-            dma(2, heads), dma(4, heads), pltpu.SemaphoreType.REGULAR,
+            dma(span, 2, heads), dma(span, heads), dma(span, heads), dma(span, 4, heads),
+            dma(2, heads), dma(4, heads), pltpu.SemaphoreType.REGULAR((4,)),
         ],
         compiler_params=pltpu.CompilerParams(collective_id=0, has_side_effects=True),
         name="log_linear",

time: 87.6 us -> 96.8 us (1.11)
  Pallas kernels: 82 us -> 91.2 us
    pallas_call x1, Pallas kernels: 82 us -> 91.2 us  [on_device(): pl.pallas_call(functools.partial(kernel, n_seq, heads, length, half_d), o...]
where the time goes in v3:
time: 96.8 us; the launch traced here: 96.7 us
  Pallas kernels  91.2 us (94%)
  local copies, waits for them, and re-layouts  4.77 us (5%)
    pallas_call x1, Pallas kernels, on_device(): pl.pallas_call(functools.partial(kernel, n_seq, heads, length, half_d), o...  91.2 us
    unnamed x10, local copies, waits for them, and re-layouts  4.77 us

profile of v3, /device:TPU:160, one launch (start us, length us, event | category | flops | bytes accessed | tf_op | source)
XLA Modules:
  0.0 96.7 jit_solution(12555260750531256729)
XLA Ops:
  0.6 91.2 %log_linear.1 = (bf16[1,512,1024]{2,1,0:T(8,128)(2,1)}, bf16[1,512,512]{2,1,0:T(8,128)(2,1)}, bf16[1,512,512]{2,1,0:T(8,128)(2,1)}, bf16[1,512,512]{2,1,0:T(8,128)(2,1)}) custom-call(bf16[1,512,512]{2,1,0:T(8,128)(2,1)} %q_hbm.1, bf16[1,512,512]{2,1,0:T(8,128)(2,1)} %k_hbm.1, bf16[1,512,512]{2,1,0:T(8,128)(2,1)} %v_hbm.1, s32[1,16,512]{2,1,0:T(8,128)} %bitcast.1, ...), custom_call_target="tpu_custom_call" | custom-call | tf_op jit(solution)/shard_map/log_linear/pallas_call | solution.py:664
  91.9 0.0 copy-start.2
  91.9 0.0 copy-start.1
  91.9 0.0 copy-start
  91.9 2.4 %copy.14 = bf16[1,512,1024]{2,1,0:T(8,128)(2,1)} copy(bf16[1,512,1024]{2,1,0:T(8,128)(2,1)} %get-tuple-element.8) | data formatting | bytes 2097152
  94.3 0.0 copy-done.2
  94.3 0.8 copy.15
  95.1 0.0 copy-done.1
  95.1 0.8 copy.16
  95.9 0.0 copy-done
  95.9 0.8 copy.17
Async XLA Ops:
  91.9 2.4 %copy-start.2 = (bf16[1,512,512]{2,1,0:T(8,128)(2,1)S(1)}, bf16[1,512,512]{2,1,0:T(8,128)(2,1)}, u32[]{:S(2)}) copy-start(bf16[1,512,512]{2,1,0:T(8,128)(2,1)} %get-tuple-element.9) | copy-start | bytes 1572868
  91.9 3.2 %copy-start.1 = (bf16[1,512,512]{2,1,0:T(8,128)(2,1)S(1)}, bf16[1,512,512]{2,1,0:T(8,128)(2,1)}, u32[]{:S(2)}) copy-start(bf16[1,512,512]{2,1,0:T(8,128)(2,1)} %get-tuple-element.10) | copy-start | bytes 1572868
  91.9 4.0 %copy-start = (bf16[1,512,512]{2,1,0:T(8,128)(2,1)S(1)}, bf16[1,512,512]{2,1,0:T(8,128)(2,1)}, u32[]{:S(2)}) copy-start(bf16[1,512,512]{2,1,0:T(8,128)(2,1)} %get-tuple-element.11) | copy-start | bytes 1572868

commit v4 on v3

--- a/solution.py
+++ b/solution.py
@@ -61,10 +61,11 @@
 
     barrier = pltpu.get_barrier_semaphore()
     dists = (1, 2, 4)
+    third = r == 3
     pl.semaphore_signal(barrier, inc=1, device_id={"head": other}, device_id_type=MESH)
-    for d in dists:
-
-        @pl.when(n + d < n_seq)
+    for d, cond in ((1, n >= 0), (2, r == 1), (3, third), (4, third)):
+
+        @pl.when(jnp.logical_and(cond, n + d < n_seq))
         def _():
             pl.semaphore_signal(barrier, inc=1, device_id={"seq": n + d}, device_id_type=MESH)
 
@@ -90,7 +91,10 @@
         loads[i].start()
 
     one = lambda cond: cond.astype(jnp.int32)
-    pl.semaphore_wait(barrier, 1 + one(n >= 1) + one(n >= 2) + one(n >= 4) + 2 * one(end) + one(inner >= 14))
+    far_lower = one(jnp.logical_and(r >= 2, n >= 4))
+    pl.semaphore_wait(
+        barrier, 1 + one(n >= 1) + one(third) + far_lower + one(inner >= 14) + 2 * one(end)
+    )
 
     own_cols = pl.ds(pl.multiple_of(core * half_d, HD), half_d)
     other_cols = pl.ds(pl.multiple_of(other * half_d, HD), half_d)
@@ -107,7 +111,7 @@
     w_copy.start()
     for i, d in enumerate(dists):
 
-        @pl.when(n >= d)
+        @pl.when(jnp.logical_and(n >= d, third if d > 1 else n >= 0))
         def _():
             pl.semaphore_signal(ready.at[i], inc=1, device_id={"seq": n - d}, device_id_type=MESH)
 
@@ -195,7 +199,9 @@
     )
 
     def upper_in(i, cond):
-        @pl.when(jnp.logical_and(cond, n + dists[i] < n_seq))
+        mine = (n >= 0, r == 1, third)[i]
+
+        @pl.when(jnp.logical_and(jnp.logical_and(cond, mine), n + dists[i] < n_seq))
         def _():
             pl.semaphore_wait(ready.at[i], 1)
 
@@ -292,6 +298,7 @@
             for c in range(heads):
                 out[top_level, c] = joined(c, (1, 0, 2, 3)).astype(BF16)
                 umsg(1, 3, c, 1).start()
+            for c in range(heads):
                 umsg(0, 3, c, 4).start()
 
     next_level = top_level - 1
@@ -651,6 +658,20 @@
         store.wait()
 
 
+def settle(pieces, *refs):
+    sources, outs, went = refs[:4], refs[4:8], refs[8]
+    copies = [
+        pltpu.make_async_copy(
+            sources[which].at[0, pl.ds(at, rows)], outs[which].at[0, pl.ds(at, rows)], went.at[i]
+        )
+        for i, (which, at, rows) in enumerate(pieces)
+    ]
+    for copy in copies:
+        copy.start()
+    for copy in copies:
+        copy.wait()
+
+
 def on_device(query_in, key_in, value_in, level_mask, out_weight, grad_out):
     n_seq = lax.axis_size("seq")
     _, length, width = query_in.shape
@@ -669,7 +690,7 @@
             jax.ShapeDtypeStruct(query_in.shape, BF16),
             jax.ShapeDtypeStruct(query_in.shape, BF16),
         ),
-        in_specs=[any_spec] * 6,
+        in_specs=[pl.BlockSpec(memory_space=pltpu.HBM)] * 6,
         out_specs=(any_spec,) * 4,
         scratch_shapes=[
             wide(BF16), wide(BF16), wide(BF16),
@@ -699,10 +720,21 @@
             dma(span, 2, heads), dma(span, heads), dma(span, heads), dma(span, 4, heads),
             dma(2, heads), dma(4, heads), pltpu.SemaphoreType.REGULAR((4,)),
         ],
-        compiler_params=pltpu.CompilerParams(collective_id=0, has_side_effects=True),
+        compiler_params=pltpu.CompilerParams(collective_id=0, has_side_effects=True, vmem_limit_bytes=57 << 20),
         name="log_linear",
     )(query_in, key_in, value_in, jnp.swapaxes(level_mask, 1, 2), out_weight, grad_out)
-    return layer, gq, gk, gv
+    results = (layer, gq, gk, gv)
+    pieces = [(0, i * length // 4, length // 4) for i in range(4)]
+    pieces += [(which, i * half, half) for which in (1, 2, 3) for i in range(2)]
+    return pl.pallas_call(
+        functools.partial(settle, pieces),
+        out_shape=tuple(jax.ShapeDtypeStruct(x.shape, x.dtype) for x in results),
+        in_specs=[any_spec] * 4,
+        out_specs=(any_spec,) * 4,
+        scratch_shapes=[dma(len(pieces))],
+        compiler_params=pltpu.CompilerParams(vmem_limit_bytes=8 << 20),
+        name="settle",
+    )(*results)
 
 
 def solution(mesh):

time: 96.8 us -> 82.6 us (0.85)
  Pallas kernels: 91.2 us -> 77.3 us
    pallas_call x1, Pallas kernels: 91.2 us -> 75.8 us  [on_device(): pl.pallas_call(functools.partial(kernel, n_seq, heads, length, half_d), o...]
    pallas_call x0 -> x1, Pallas kernels: none -> 1.56 us  [on_device(): pl.pallas_call(functools.partial(settle, pieces), out_shape=tuple((jax.Sh...]
    unnamed x10 -> x8, local copies, waits for them, and re-layouts: 4.77 us -> 4.34 us
where the time goes in v4:
time: 82.6 us; the launch traced here: 82.3 us
  Pallas kernels  77.3 us (94%)
  local copies, waits for them, and re-layouts  4.34 us (5%)
    pallas_call x1, Pallas kernels, on_device(): pl.pallas_call(functools.partial(kernel, n_seq, heads, length, half_d), o...  75.8 us
    unnamed x8, local copies, waits for them, and re-layouts  4.34 us

profile of v4, /device:TPU:160, one launch (start us, length us, event | category | flops | bytes accessed | tf_op | source)
XLA Modules:
  0.0 82.3 jit_solution(15370740044577582164)
XLA Ops:
  0.6 75.8 %log_linear.1 = (bf16[1,512,1024]{2,1,0:T(8,128)(2,1)}, bf16[1,512,512]{2,1,0:T(8,128)(2,1)}, bf16[1,512,512]{2,1,0:T(8,128)(2,1)}, bf16[1,512,512]{2,1,0:T(8,128)(2,1)}) custom-call(bf16[1,512,512]{2,1,0:T(8,128)(2,1)} %q_hbm.1, bf16[1,512,512]{2,1,0:T(8,128)(2,1)} %k_hbm.1, bf16[1,512,512]{2,1,0:T(8,128)(2,1)} %v_hbm.1, s32[1,16,512]{2,1,0:T(8,128)} %bitcast.1, ...), custom_call_target="tpu_custom_call" | custom-call | tf_op jit(solution)/shard_map/log_linear/pallas_call | solution.py:685
  76.4 0.0 copy-start
  76.4 1.2 %copy-done = bf16[1,512,1024]{2,1,0:T(8,128)(2,1)S(1)} copy-done((bf16[1,512,1024]{2,1,0:T(8,128)(2,1)S(1)}, bf16[1,512,1024]{2,1,0:T(8,128)(2,1)}, u32[]{:S(2)}) %copy-start) | copy-done | bytes 1048600
  77.6 0.0 copy-start.1
  77.6 1.0 %copy-done.1 = bf16[1,512,512]{2,1,0:T(8,128)(2,1)S(1)} copy-done((bf16[1,512,512]{2,1,0:T(8,128)(2,1)S(1)}, bf16[1,512,512]{2,1,0:T(8,128)(2,1)}, u32[]{:S(2)}) %copy-start.1) | copy-done | bytes 524312
  78.7 0.0 copy-start.2
  78.7 1.0 %copy-done.2 = bf16[1,512,512]{2,1,0:T(8,128)(2,1)S(1)} copy-done((bf16[1,512,512]{2,1,0:T(8,128)(2,1)S(1)}, bf16[1,512,512]{2,1,0:T(8,128)(2,1)}, u32[]{:S(2)}) %copy-start.2) | copy-done | bytes 524312
  79.7 0.0 copy-start.3
  79.7 1.0 %copy-done.3 = bf16[1,512,512]{2,1,0:T(8,128)(2,1)S(1)} copy-done((bf16[1,512,512]{2,1,0:T(8,128)(2,1)S(1)}, bf16[1,512,512]{2,1,0:T(8,128)(2,1)}, u32[]{:S(2)}) %copy-start.3) | copy-done | bytes 524312
  80.8 1.6 %settle.1 = (bf16[1,512,1024]{2,1,0:T(8,128)(2,1)}, bf16[1,512,512]{2,1,0:T(8,128)(2,1)}, bf16[1,512,512]{2,1,0:T(8,128)(2,1)}, bf16[1,512,512]{2,1,0:T(8,128)(2,1)}) custom-call(bf16[1,512,1024]{2,1,0:T(8,128)(2,1)S(1)} %copy-done, bf16[1,512,512]{2,1,0:T(8,128)(2,1)S(1)} %copy-done.1, bf16[1,512,512]{2,1,0:T(8,128)(2,1)S(1)} %copy-done.2, ...), custom_call_target="tpu_custom_call" | custom-call | tf_op jit(solution)/shard_map/settle/pallas_call | solution.py:729
Async XLA Ops:
  76.4 1.2 %copy-start = (bf16[1,512,1024]{2,1,0:T(8,128)(2,1)S(1)}, bf16[1,512,1024]{2,1,0:T(8,128)(2,1)}, u32[]{:S(2)}) copy-start(bf16[1,512,1024]{2,1,0:T(8,128)(2,1)} %get-tuple-element.8.refs_0_) | copy-start | bytes 3145732
  77.6 1.0 %copy-start.1 = (bf16[1,512,512]{2,1,0:T(8,128)(2,1)S(1)}, bf16[1,512,512]{2,1,0:T(8,128)(2,1)}, u32[]{:S(2)}) copy-start(bf16[1,512,512]{2,1,0:T(8,128)(2,1)} %get-tuple-element.9.refs_1_) | copy-start | bytes 1572868
  78.7 1.0 %copy-start.2 = (bf16[1,512,512]{2,1,0:T(8,128)(2,1)S(1)}, bf16[1,512,512]{2,1,0:T(8,128)(2,1)}, u32[]{:S(2)}) copy-start(bf16[1,512,512]{2,1,0:T(8,128)(2,1)} %get-tuple-element.10.refs_2_) | copy-start | bytes 1572868
  79.7 1.0 %copy-start.3 = (bf16[1,512,512]{2,1,0:T(8,128)(2,1)S(1)}, bf16[1,512,512]{2,1,0:T(8,128)(2,1)}, u32[]{:S(2)}) copy-start(bf16[1,512,512]{2,1,0:T(8,128)(2,1)} %get-tuple-element.11.refs_3_) | copy-start | bytes 1572868

commit v5 on v4

--- a/solution.py
+++ b/solution.py
@@ -408,8 +408,8 @@
     def down(level):
         return {0: (0, 1), 1: (1, 2)}.get(level, (1, 4))
 
-    def back_step(j):
-        @pl.when(jnp.logical_and(jnp.logical_and(r == 3, after[j] == 1), up[j] == 0))
+    def back_step(j, where):
+        @pl.when(jnp.logical_and(jnp.logical_and(where, after[j] == 1), up[j] == 0))
         def _():
             slot, dist = down(j - 1)
             for c in range(heads):
@@ -457,6 +457,15 @@
         local_head(i)
         return carry
 
+    @pl.when(r == 1)
+    def _():
+        for c in range(heads):
+            fwait(0, c)
+            agg[c] = (state[c] + fr[0, c].astype(F32)).astype(BF16)
+            fsend(1, 0, c, agg.at[c], 2)
+        for c in range(heads):
+            fsend(1, 1, c, agg.at[c], 1)
+
     lax.fori_loop(0, heads, local_body, 0)
 
     def bsent(cond, level):
@@ -487,16 +496,10 @@
     chain_step(2, r == 1, 2, -1)
     chain_step(2, r == 2, 0, 3)
 
-    @pl.when(r == 1)
-    def _():
-        for c in range(heads):
-            fwait(0, c)
-            agg[c] = (state[c] + fr[0, c].astype(F32)).astype(BF16)
-            fsend(1, 0, c, agg.at[c], 2)
-            fsend(1, 1, c, agg.at[c], 1)
-
     def source_of(level):
         return jnp.logical_and(nxt[level] == 1, up[level] == 0)
+
+    back_step(2, n == 3)
 
     @pl.when(r == 3)
     def _():
@@ -516,7 +519,7 @@
                 fsend(2, 1, c, agg.at[c], 1)
 
     for j in (3, 2):
-        back_step(j)
+        back_step(j, jnp.logical_and(r == 3, n != 3))
 
     @pl.when(r == 1)
     def _():
@@ -659,17 +662,19 @@
 
 
 def settle(pieces, *refs):
-    sources, outs, went = refs[:4], refs[4:8], refs[8]
-    copies = [
-        pltpu.make_async_copy(
-            sources[which].at[0, pl.ds(at, rows)], outs[which].at[0, pl.ds(at, rows)], went.at[i]
-        )
-        for i, (which, at, rows) in enumerate(pieces)
-    ]
-    for copy in copies:
-        copy.start()
-    for copy in copies:
-        copy.wait()
+    sources, outs, held = refs[:4], refs[4:8], refs[8:12]
+    came, went = refs[12], refs[13]
+    into, back = [], []
+    for i, (which, at, rows) in enumerate(pieces):
+        here = pl.ds(at, rows)
+        into.append(pltpu.make_async_copy(sources[which].at[0, here], held[which].at[here], came.at[i]))
+        back.append(pltpu.make_async_copy(held[which].at[here], outs[which].at[0, here], went.at[i]))
+        into[-1].start()
+    for i in range(len(pieces)):
+        into[i].wait()
+        back[i].start()
+    for i in range(len(pieces)):
+        back[i].wait()
 
 
 def on_device(query_in, key_in, value_in, level_mask, out_weight, grad_out):
@@ -720,7 +725,7 @@
             dma(span, 2, heads), dma(span, heads), dma(span, heads), dma(span, 4, heads),
             dma(2, heads), dma(4, heads), pltpu.SemaphoreType.REGULAR((4,)),
         ],
-        compiler_params=pltpu.CompilerParams(collective_id=0, has_side_effects=True, vmem_limit_bytes=57 << 20),
+        compiler_params=pltpu.CompilerParams(collective_id=0, has_side_effects=True),
         name="log_linear",
     )(query_in, key_in, value_in, jnp.swapaxes(level_mask, 1, 2), out_weight, grad_out)
     results = (layer, gq, gk, gv)
@@ -731,8 +736,8 @@
         out_shape=tuple(jax.ShapeDtypeStruct(x.shape, x.dtype) for x in results),
         in_specs=[any_spec] * 4,
         out_specs=(any_spec,) * 4,
-        scratch_shapes=[dma(len(pieces))],
-        compiler_params=pltpu.CompilerParams(vmem_limit_bytes=8 << 20),
+        scratch_shapes=[pltpu.VMEM(x.shape[1:], x.dtype) for x in results]
+        + [dma(len(pieces)), dma(len(pieces))],
         name="settle",
     )(*results)
 

time: 82.6 us -> 75 us (0.908)
  the two profiles are of different devices: /device:TPU:160 before, /device:TPU:1963 now
where the time goes in v5:
time: 75 us; the launch traced here: 74.8 us
  Pallas kernels  74.2 us (99%)
    pallas_call x1, Pallas kernels, on_device(): pl.pallas_call(functools.partial(kernel, n_seq, heads, length, half_d), o...  71.6 us
    pallas_call x1, Pallas kernels, on_device(): pl.pallas_call(functools.partial(settle, pieces), out_shape=tuple((jax.Sh...  2.6 us

profile of v5, /device:TPU:1963, one launch (start us, length us, event | category | flops | bytes accessed | tf_op | source)
XLA Modules:
  0.0 74.8 jit_solution(9520217829811807822)
XLA Ops:
  0.6 71.6 %log_linear.1 = (bf16[1,512,1024]{2,1,0:T(8,128)(2,1)}, bf16[1,512,512]{2,1,0:T(8,128)(2,1)}, bf16[1,512,512]{2,1,0:T(8,128)(2,1)}, bf16[1,512,512]{2,1,0:T(8,128)(2,1)}) custom-call(bf16[1,512,512]{2,1,0:T(8,128)(2,1)} %q_hbm.1, bf16[1,512,512]{2,1,0:T(8,128)(2,1)} %k_hbm.1, bf16[1,512,512]{2,1,0:T(8,128)(2,1)} %v_hbm.1, s32[1,16,512]{2,1,0:T(8,128)} %bitcast.1, ...), custom_call_target="tpu_custom_call" | custom-call | tf_op jit(solution)/shard_map/log_linear/pallas_call | solution.py:690
  72.2 2.6 %settle.1 = (bf16[1,512,1024]{2,1,0:T(8,128)(2,1)}, bf16[1,512,512]{2,1,0:T(8,128)(2,1)}, bf16[1,512,512]{2,1,0:T(8,128)(2,1)}, bf16[1,512,512]{2,1,0:T(8,128)(2,1)}) custom-call(bf16[1,512,1024]{2,1,0:T(8,128)(2,1)} %get-tuple-element.8.refs_0_, bf16[1,512,512]{2,1,0:T(8,128)(2,1)} %get-tuple-element.9.refs_1_, ...), custom_call_target="tpu_custom_call" | custom-call | tf_op jit(solution)/shard_map/settle/pallas_call | solution.py:734
